TPU v7x, 64 devices: a 2x2x8 block of a 4x4x8 slice. The times are simulated.
64 devices in a mesh: dp: 4 (over x, y), tp: 16 (over z, core).
Axes of the slice: x: 2, y: 2, z: 8, core: 2. Of those that a mesh axis runs over, the one named last changes fastest.
The devices are a block of a 4x4x8 slice.
Arguments:
- x_in: bfloat16 [8192, 2048], P(('dp', 'tp')), parts along dimension 0
- grad_y: bfloat16 [8192, 2048], P(('dp', 'tp')), parts along dimension 0
- norm_gain: float32 [2, 2048], replicated
- w_qkv: bfloat16 [2, 2048, 6144], P(None, None, 'tp')
- w_out: bfloat16 [2, 2048, 2048], P(None, 'tp')
- w_gate: bfloat16 [2, 2048, 8192], P(None, None, 'tp')
- w_up: bfloat16 [2, 2048, 8192], P(None, None, 'tp')
- w_down: bfloat16 [2, 8192, 2048], P(None, 'tp')
Outputs:
- output 1: bfloat16 [8192, 2048], P(('dp', 'tp')), parts along dimension 0
- output 2: float32 [8, 2048], P('dp'), parts along dimension 0
- output 3: bfloat16 [8, 2048, 6144], P('dp', None, 'tp'), parts along dimension 0
- output 4: bfloat16 [8, 2048, 2048], P('dp', 'tp'), parts along dimension 0
- output 5: bfloat16 [8, 2048, 8192], P('dp', None, 'tp'), parts along dimension 0
- output 6: bfloat16 [8, 2048, 8192], P('dp', None, 'tp'), parts along dimension 0
- output 7: bfloat16 [8, 8192, 2048], P('dp', 'tp'), parts along dimension 0
There are 4 independent parts. A program takes and returns all parts, laid end to end along the dimension named above; an argument that names none is the same for every part.
All inputs are finite; a program needn't handle non-finite values.
Results may differ from a plain program's by a relative error of at most 0.0158805.
Values are sent between devices in bfloat16 or wider.
A program may use at most 768 MiB of HBM per device.

v0:
```python
import jax
import jax.numpy as jnp
from jax import lax
from jax.sharding import PartitionSpec as P

HEAD_DIM = 128
NORM_EPS = 1e-5
ROPE_BASE = 10000.0


def rope_tables(seq_len):
    half_dim = HEAD_DIM // 2
    freqs = ROPE_BASE ** (-2.0 * jnp.arange(half_dim, dtype=jnp.float32) / HEAD_DIM)
    angles = jnp.arange(seq_len, dtype=jnp.float32)[:, None] * freqs[None, :]
    return jnp.cos(angles)[:, None, None, :], jnp.sin(angles)[:, None, None, :]


def rotate(values, cos_tab, sin_tab):
    half_dim = values.shape[-1] // 2
    lower_half = values[..., :half_dim]
    upper_half = values[..., half_dim:]
    return jnp.concatenate([lower_half * cos_tab - upper_half * sin_tab, upper_half * cos_tab + lower_half * sin_tab], axis=-1)


def rms_scale(x_f32, gain_row):
    inv_rms = lax.rsqrt(jnp.mean(x_f32 * x_f32, axis=-1, keepdims=True) + NORM_EPS)
    return x_f32 * inv_rms * gain_row


def gated(gate_f32, up_f32):
    return jax.nn.silu(gate_f32) * up_f32


def causal_scores(query, keys_rot):
    seq_len = query.shape[0]
    causal = jnp.arange(seq_len)[:, None] >= jnp.arange(seq_len)[None, :]
    scores = jnp.einsum('skgd,tkd->kgst', query, keys_rot, preferred_element_type=jnp.float32) * HEAD_DIM ** -0.5
    return jnp.where(causal, scores, -1e30)


def block_forward(x_loc, gain_row, w_qkv_l, w_out_l, w_gate_l, w_up_l, w_down_l, cos_tab, sin_tab, with_output):
    seq_len = cos_tab.shape[0]
    heads_local = w_out_l.shape[0] // HEAD_DIM
    kv_local = (w_qkv_l.shape[1] // HEAD_DIM - heads_local) // 2
    group_size = heads_local // kv_local
    x_f32 = x_loc.astype(jnp.float32)
    u_loc = rms_scale(x_f32, gain_row).astype(jnp.bfloat16)
    u_full = lax.all_gather(u_loc, 'tp', axis=0, tiled=True)
    qkv_all = jnp.dot(u_full, w_qkv_l, preferred_element_type=jnp.float32).astype(jnp.bfloat16).reshape(seq_len, kv_local, group_size + 2, HEAD_DIM)
    rotated = rotate(qkv_all[:, :, :group_size + 1].astype(jnp.float32), cos_tab, sin_tab).astype(jnp.bfloat16)
    query = rotated[:, :, :group_size]
    keys_rot = rotated[:, :, group_size]
    values_v = qkv_all[:, :, group_size + 1]
    scores = causal_scores(query, keys_rot)
    row_max = jnp.max(scores, axis=-1, keepdims=True)
    log_norm = row_max + jnp.log(jnp.sum(jnp.exp(scores - row_max), axis=-1, keepdims=True))
    attn_prob = jnp.exp(scores - log_norm).astype(jnp.bfloat16)
    attn_out = jnp.einsum('kgst,tkd->skgd', attn_prob, values_v, preferred_element_type=jnp.float32).astype(jnp.bfloat16).reshape(seq_len, heads_local * HEAD_DIM)
    gate_act = jnp.dot(u_full, w_gate_l, preferred_element_type=jnp.float32).astype(jnp.bfloat16)
    up_act = jnp.dot(u_full, w_up_l, preferred_element_type=jnp.float32).astype(jnp.bfloat16)
    saved = {'x_loc': x_loc, 'u_loc': u_loc, 'query': query, 'keys_rot': keys_rot, 'values_v': values_v, 'attn_out': attn_out, 'log_norm': log_norm, 'gate_act': gate_act, 'up_act': up_act}
    if not with_output:
        return None, saved
    hidden = gated(gate_act.astype(jnp.float32), up_act.astype(jnp.float32)).astype(jnp.bfloat16)
    block_part = jnp.dot(attn_out, w_out_l, preferred_element_type=jnp.float32) + jnp.dot(hidden, w_down_l, preferred_element_type=jnp.float32)
    y_loc = (x_f32 + lax.psum_scatter(block_part, 'tp', scatter_dimension=0, tiled=True)).astype(jnp.bfloat16)
    return y_loc, saved


def block_backward(dy_loc, saved, gain_row, w_qkv_l, w_out_l, w_gate_l, w_up_l, w_down_l, cos_tab, sin_tab):
    saved, dy_loc = lax.optimization_barrier((saved, dy_loc))
    query = saved['query']
    keys_rot = saved['keys_rot']
    values_v = saved['values_v']
    seq_len, kv_local, group_size = query.shape[0], query.shape[1], query.shape[2]
    u_full = lax.all_gather(saved['u_loc'], 'tp', axis=0, tiled=True)
    dy_full = lax.all_gather(dy_loc, 'tp', axis=0, tiled=True)
    grad_out_l = jnp.einsum('sh,sd->hd', saved['attn_out'], dy_full, preferred_element_type=jnp.float32).astype(jnp.bfloat16)
    d_attn = jnp.einsum('sd,hd->sh', dy_full, w_out_l, preferred_element_type=jnp.float32).astype(jnp.bfloat16).reshape(seq_len, kv_local, group_size, HEAD_DIM)
    hidden_f32, gated_pull = jax.vjp(gated, saved['gate_act'].astype(jnp.float32), saved['up_act'].astype(jnp.float32))
    hidden = hidden_f32.astype(jnp.bfloat16)
    grad_down_l = jnp.einsum('sf,sd->fd', hidden, dy_full, preferred_element_type=jnp.float32).astype(jnp.bfloat16)
    d_hidden = jnp.einsum('sd,fd->sf', dy_full, w_down_l, preferred_element_type=jnp.float32).astype(jnp.bfloat16)
    d_gate_f32, d_up_f32 = gated_pull(d_hidden.astype(jnp.float32))
    d_gate = d_gate_f32.astype(jnp.bfloat16)
    d_up = d_up_f32.astype(jnp.bfloat16)
    grad_gate_l = jnp.einsum('sd,sf->df', u_full, d_gate, preferred_element_type=jnp.float32).astype(jnp.bfloat16)
    grad_up_l = jnp.einsum('sd,sf->df', u_full, d_up, preferred_element_type=jnp.float32).astype(jnp.bfloat16)
    attn_prob_f32 = jnp.exp(causal_scores(query, keys_rot) - saved['log_norm'])
    attn_prob = attn_prob_f32.astype(jnp.bfloat16)
    d_values = jnp.einsum('kgst,skgd->tkd', attn_prob, d_attn, preferred_element_type=jnp.float32).astype(jnp.bfloat16)
    d_prob = jnp.einsum('skgd,tkd->kgst', d_attn, values_v, preferred_element_type=jnp.float32).astype(jnp.bfloat16).astype(jnp.float32)
    d_scores = (attn_prob_f32 * (d_prob - jnp.sum(attn_prob_f32 * d_prob, axis=-1, keepdims=True)) * HEAD_DIM ** -0.5).astype(jnp.bfloat16)
    d_query = jnp.einsum('kgst,tkd->skgd', d_scores, keys_rot, preferred_element_type=jnp.float32).astype(jnp.bfloat16)
    d_keys = jnp.einsum('kgst,skgd->tkd', d_scores, query, preferred_element_type=jnp.float32).astype(jnp.bfloat16)
    d_rotated = jnp.concatenate([d_query, d_keys[:, :, None]], axis=2).astype(jnp.float32)
    d_unrotated = rotate(d_rotated, cos_tab, -sin_tab).astype(jnp.bfloat16)
    d_qkv = jnp.concatenate([d_unrotated, d_values[:, :, None]], axis=2).reshape(seq_len, w_qkv_l.shape[1])
    grad_qkv_l = jnp.einsum('sd,sc->dc', u_full, d_qkv, preferred_element_type=jnp.float32).astype(jnp.bfloat16)
    normed_part = jnp.einsum('sc,dc->sd', d_qkv, w_qkv_l, preferred_element_type=jnp.float32) + jnp.einsum('sf,df->sd', d_gate, w_gate_l, preferred_element_type=jnp.float32) + jnp.einsum('sf,df->sd', d_up, w_up_l, preferred_element_type=jnp.float32)
    d_normed = lax.psum_scatter(normed_part, 'tp', scatter_dimension=0, tiled=True).astype(jnp.bfloat16)
    norm_pull = jax.vjp(rms_scale, saved['x_loc'].astype(jnp.float32), gain_row)[1]
    d_x_norm, grad_gain_l = norm_pull(d_normed.astype(jnp.float32))
    grad_x_loc = (dy_loc.astype(jnp.float32) + d_x_norm).astype(jnp.bfloat16)
    return grad_x_loc, grad_gain_l, grad_qkv_l, grad_out_l, grad_gate_l, grad_up_l, grad_down_l


def solution(mesh):
    tp_size = mesh.shape['tp']
    row_spec = P(('dp', 'tp'), None)
    col_spec = P(None, None, 'tp')
    inner_spec = P(None, 'tp', None)

    def device_program(x_loc, dy_loc, norm_gain, w_qkv, w_out, w_gate, w_up, w_down):
        n_layers = w_qkv.shape[0]
        cos_tab, sin_tab = rope_tables(x_loc.shape[0] * tp_size)
        saved_all = []
        x_cur = x_loc
        for layer_idx in range(n_layers):
            x_cur, saved = block_forward(x_cur, norm_gain[layer_idx], w_qkv[layer_idx], w_out[layer_idx], w_gate[layer_idx], w_up[layer_idx], w_down[layer_idx], cos_tab, sin_tab, layer_idx < n_layers - 1)
            saved_all.append(saved)
        grad_cur = dy_loc
        layer_grads = []
        for layer_idx in reversed(range(n_layers)):
            results = block_backward(grad_cur, saved_all[layer_idx], norm_gain[layer_idx], w_qkv[layer_idx], w_out[layer_idx], w_gate[layer_idx], w_up[layer_idx], w_down[layer_idx], cos_tab, sin_tab)
            grad_cur = results[0]
            layer_grads.insert(0, results[1:])
        grad_gain = lax.psum(jnp.stack([item[0] for item in layer_grads]), 'tp')
        stacked = [jnp.stack([item[grad_idx] for item in layer_grads]) for grad_idx in range(1, 6)]
        return (grad_cur, grad_gain, stacked[0], stacked[1], stacked[2], stacked[3], stacked[4])

    return jax.shard_map(device_program, mesh=mesh, in_specs=(row_spec, row_spec, P(None, None), col_spec, inner_spec, col_spec, col_spec, inner_spec), out_specs=(row_spec, P('dp', None), P('dp', None, 'tp'), P('dp', 'tp', None), P('dp', None, 'tp'), P('dp', None, 'tp'), P('dp', 'tp', None)), check_vma=False)
```

profile of v0, /device:TPU:21, one launch (start us, length us, event | category | flops | bytes accessed | tf_op | source)
XLA Modules:
  0.0 843.3 jit_solution(6315435260921437332)
XLA Ops:
  14.2 54.8 %all-gather.7.cloned.1.call-done = bf16[2048,2048]{1,0:T(8,128)(2,1)} async-done(((bf16[128,2048]{1,0:T(8,128)(2,1)}), bf16[2048,2048]{1,0:T(8,128)(2,1)}) %all-gather.7.cloned.1.call-update) | async-done | bytes 8388624 | tf_op jit(solution)/shard_map/all_gather | solution.py:48
  90.3 8.7 %convolution_convert_fusion.12 = bf16[2048,512]{1,0:T(8,128)(2,1)S(1)} fusion(bf16[2048,2048]{1,0:T(8,128)(2,1)} %all-gather.7.cloned.1.call-done, bf16[2,2048,512]{2,1,0:T(8,128)(2,1)} %param.14), kind=kOutput, calls=%fused_computation.97 | convolution fusion | flops 4296015872 | bytes 12582912 | tf_op jit(solution)/shard_map/dot_general | solution.py:60
  111.9 8.2 convolution_add_fusion
  120.2 94.9 %reduce-scatter.4.cloned.1.call-done = f32[128,2048]{1,0:T(8,128)} async-done(((f32[2048,2048]{1,0:T(8,128)}), f32[128,2048]{1,0:T(8,128)}) %reduce-scatter.4.cloned.1.call-update) | async-done | bytes 1048592 | tf_op jit(solution)/shard_map/reduce_scatter | solution.py:66
  218.2 51.8 %all-gather.9.cloned.1.call-done = bf16[2048,2048]{1,0:T(8,128)(2,1)} async-done(((bf16[128,2048]{1,0:T(8,128)(2,1)}), bf16[2048,2048]{1,0:T(8,128)(2,1)}) %all-gather.9.cloned.1.call-update) | async-done | bytes 8388624 | tf_op jit(solution)/shard_map/all_gather | solution.py:48
  291.1 10.0 %convolution_convert_fusion.10 = bf16[2048,512]{1,0:T(8,128)(2,1)} fusion(bf16[2048,2048]{1,0:T(8,128)(2,1)} %all-gather.9.cloned.1.call-done, bf16[2,2048,512]{2,1,0:T(8,128)(2,1)} %param.14), kind=kOutput, calls=%fused_computation.95 | convolution fusion | flops 4296015872 | bytes 12582912 | tf_op jit(solution)/shard_map/dot_general | solution.py:60
  307.3 50.9 %all-gather.11.cloned.1.call-done = bf16[2048,2048]{1,0:T(8,128)(2,1)} async-done(((bf16[128,2048]{1,0:T(8,128)(2,1)}), bf16[2048,2048]{1,0:T(8,128)(2,1)}) %all-gather.11.cloned.1.call-update) | async-done | bytes 8388624 | tf_op jit(solution)/shard_map/all_gather | solution.py:77
  385.5 8.7 %convolution_convert_fusion.9 = bf16[2048,512]{1,0:T(8,128)(2,1)S(1)} fusion(bf16[2048,2048]{1,0:T(8,128)(2,1)} %all-gather.11.cloned.1.call-done, bf16[2,512,2048]{2,1,0:T(8,128)(2,1)} %param.15), kind=kOutput, calls=%fused_computation.94 | convolution fusion | flops 4296015872 | bytes 12582912 | tf_op jit(solution)/shard_map/sd,fd->sf/dot_general | solution.py:83
  394.2 8.9 %fusion.96 = f32[2048,2048]{1,0:T(8,128)} fusion(bf16[2,2048,512]{2,1,0:T(8,128)(2,1)S(1)} %copy-done.32, bf16[2048,512]{1,0:T(8,128)(2,1)S(1)} %convolution_convert_fusion.9, bf16[2048,512]{1,0:T(8,128)(2,1)S(1)} %copy-done.43), kind=kOutput, calls=%fused_computation.135 | convolution fusion | flops 4303355904 | bytes 23068672 | tf_op jit(solution)/shard_map/sf,df->sd/dot_general | solution.py:100
  403.1 9.1 %fusion.99 = f32[2048,2048]{1,0:T(8,128)} fusion(bf16[2,2048,512]{2,1,0:T(8,128)(2,1)S(1)} %copy-done.36, bf16[2048,512]{1,0:T(8,128)(2,1)S(1)} %copy-done.43, bf16[2048,512]{1,0:T(8,128)(2,1)S(1)} %copy-done.49, bf16[2048,512]{1,0:T(8,128)(2,1)S(1)} %convolution_convert_fusion.9), kind=kOutput, calls=%fused_computation.138 | convolution fusion | flops 4309647360 | bytes 25165824 | tf_op jit(solution)/shard_map/sf,df->sd/dot_general | solution.py:100
  413.4 19.7 %add_add_fusion.1 = f32[2048,2048]{1,0:T(8,128)} fusion(f32[2048,2048]{1,0:T(8,128)} %fusion.96, f32[2048,2048]{1,0:T(8,128)} %fusion.99, bf16[2048,384]{0,1:T(8,128)(2,1)S(1)} %bitcast.349, bf16[2,2048,384]{2,1,0:T(8,128)(2,1)} %param.11), kind=kOutput, calls=%fused_computation.23 | convolution fusion | flops 3229614080 | bytes 53477376 | tf_op jit(solution)/shard_map/sc,dc->sd/dot_general | solution.py:100
  435.3 92.8 %reduce-scatter.6.cloned.1.call-done = f32[128,2048]{1,0:T(8,128)} async-done(((f32[2048,2048]{1,0:T(8,128)}), f32[128,2048]{1,0:T(8,128)}) %reduce-scatter.6.cloned.1.call-update) | async-done | bytes 1048592 | tf_op jit(solution)/shard_map/reduce_scatter | solution.py:101
  534.9 50.4 %all-gather.13.cloned.1.call-done = bf16[2048,2048]{1,0:T(8,128)(2,1)} async-done(((bf16[128,2048]{1,0:T(8,128)(2,1)}), bf16[2048,2048]{1,0:T(8,128)(2,1)}) %all-gather.13.cloned.1.call-update) | async-done | bytes 8388624 | tf_op jit(solution)/shard_map/all_gather | solution.py:77
  594.8 8.0 fusion.6
  623.8 9.1 %convolution_convert_fusion.8 = bf16[2048,512]{1,0:T(8,128)(2,1)S(1)} fusion(bf16[2048,2048]{1,0:T(8,128)(2,1)} %all-gather.13.cloned.1.call-done, bf16[2,512,2048]{2,1,0:T(8,128)(2,1)} %param.15), kind=kOutput, calls=%fused_computation.93 | convolution fusion | flops 4296015872 | bytes 12582912 | tf_op jit(solution)/shard_map/sd,fd->sf/dot_general | solution.py:83
  633.0 9.2 %fusion.104 = f32[2048,2048]{1,0:T(8,128)} fusion(bf16[2,2048,512]{2,1,0:T(8,128)(2,1)S(1)} %copy-done.33, bf16[2048,512]{1,0:T(8,128)(2,1)S(1)} %convolution_convert_fusion.8, bf16[2048,512]{1,0:T(8,128)(2,1)S(1)} %copy-done.41), kind=kOutput, calls=%fused_computation.143 | convolution fusion | flops 4303355904 | bytes 23068672 | tf_op jit(solution)/shard_map/sf,df->sd/dot_general | solution.py:100
  642.2 9.1 %fusion.107 = f32[2048,2048]{1,0:T(8,128)} fusion(bf16[2,2048,512]{2,1,0:T(8,128)(2,1)S(1)} %copy-done.37, bf16[2048,512]{1,0:T(8,128)(2,1)S(1)} %copy-done.41, bf16[2048,512]{1,0:T(8,128)(2,1)S(1)} %copy-done.39, bf16[2048,512]{1,0:T(8,128)(2,1)S(1)} %convolution_convert_fusion.8), kind=kOutput, calls=%fused_computation.146 | convolution fusion | flops 4309647360 | bytes 25165824 | tf_op jit(solution)/shard_map/sf,df->sd/dot_general | solution.py:100
  651.3 19.8 %add_add_fusion = f32[2048,2048]{1,0:T(8,128)} fusion(f32[2048,2048]{1,0:T(8,128)} %fusion.104, f32[2048,2048]{1,0:T(8,128)} %fusion.107, bf16[2048,384]{0,1:T(8,128)(2,1)S(1)} %bitcast.351, bf16[2,2048,384]{2,1,0:T(8,128)(2,1)} %param.11), kind=kOutput, calls=%fused_computation.22 | convolution fusion | flops 3229614080 | bytes 53477376 | tf_op jit(solution)/shard_map/sc,dc->sd/dot_general | solution.py:100
  677.6 9.3 %fusion.60 = bf16[1,2048,384]{2,1,0:T(8,128)(2,1)} fusion(bf16[2048,2048]{1,0:T(8,128)(2,1)} %all-gather.17.cloned.1.call-done, bf16[2048,384]{0,1:T(8,128)(2,1)S(1)} %bitcast.350), kind=kOutput, calls=%fused_computation.110 | convolution fusion | flops 3222011904 | bytes 11534336 | tf_op jit(solution)/shard_map/sd,sc->dc/dot_general | solution.py:99
  686.9 9.6 %fusion.58 = bf16[1,512,2048]{2,1,0:T(8,128)(2,1)} fusion(bf16[2048,2048]{1,0:T(8,128)(2,1)} %all-gather.11.cloned.1.call-done, bf16[2048,512]{1,0:T(8,128)(2,1)S(1)} %copy-done.50, bf16[2048,512]{1,0:T(8,128)(2,1)S(1)} %copy-done.44), kind=kOutput, calls=%fused_computation.108 | convolution fusion | flops 4304404480 | bytes 14680064 | tf_op jit(solution)/shard_map/sf,sd->fd/dot_general | solution.py:82
  713.1 8.1 fusion.59
  723.4 10.1 %fusion.57 = bf16[1,512,2048]{2,1,0:T(8,128)(2,1)S(1)} fusion(bf16[2048,2048]{1,0:T(8,128)(2,1)} %all-gather.13.cloned.1.call-done, bf16[2048,512]{1,0:T(8,128)(2,1)S(1)} %copy-done.40, bf16[2048,512]{1,0:T(8,128)(2,1)S(1)} %copy-done.42), kind=kOutput, calls=%fused_computation.107 | convolution fusion | flops 4304404480 | bytes 14680064 | tf_op jit(solution)/shard_map/sf,sd->fd/dot_general | solution.py:82
  751.4 37.0 %reduce-scatter.8.cloned.1.call-done = f32[128,2048]{1,0:T(8,128)} async-done(((f32[2048,2048]{1,0:T(8,128)}), f32[128,2048]{1,0:T(8,128)}) %reduce-scatter.8.cloned.1.call-update) | async-done | bytes 1048592 | tf_op jit(solution)/shard_map/reduce_scatter | solution.py:101
  790.1 43.8 %psum.7 = f32[2,2048]{1,0:T(2,128)} all-reduce(f32[2,2048]{1,0:T(2,128)S(1)} %pad_maximum_fusion.9), channel_id=1, replica_groups=mesh['dp'=4,'tp'=16] {'tp'}, use_global_device_ids=true, to_apply=%region_17.18 | all-reduce | flops 4096 | bytes 32768 | tf_op jit(solution)/shard_map/psum | solution.py:128
  (217 shorter events, 186.1 us)
Async XLA Ops:
  7.2 61.9 %all-gather.7.cloned.1.call-start = ((), (), s32[]{:S(2)}) async-start(), calls=%async_computation.3 | async-start | bytes 8912896 | tf_op jit(solution)/shard_map/all_gather | solution.py:48
  11.4 203.7 %reduce-scatter.4.cloned.1.call-start = ((), (), s32[]{:S(2)}) async-start(), calls=%async_computation.4 | async-start | bytes 17825792 | tf_op jit(solution)/shard_map/reduce_scatter | solution.py:66
  85.0 14.1 %slice-start.6 = ((s8[8388608]{0:T(1024)(128)(4,1)}), s8[4194304]{0:T(1024)(128)(4,1)S(1)}, s32[]{:S(2)}) async-start(s8[8388608]{0:T(1024)(128)(4,1)} %bitcast.371), calls=%async_computation.18 | async-start | bytes 8388608
  90.3 21.6 %copy-start.4 = (bf16[2048,128]{0,1:T(8,128)(2,1)}, bf16[2048,128]{0,1:T(8,128)(2,1)S(1)}, u32[]{:S(2)}) copy-start(bf16[2048,128]{0,1:T(8,128)(2,1)S(1)} %fusion.82) | copy-start | bytes 1572868
  120.0 95.0 %copy-start.2 = (bf16[128,2048]{1,0:T(8,128)(2,1)S(1)}, bf16[128,2048]{1,0:T(8,128)(2,1)}, u32[]{:S(2)}) copy-start(bf16[128,2048]{1,0:T(8,128)(2,1)} %param.8) | copy-start | bytes 1572868
  120.1 149.9 %all-gather.9.cloned.1.call-start = ((), (), s32[]{:S(2)}) async-start(), calls=%async_computation.5 | async-start | bytes 8912896 | tf_op jit(solution)/shard_map/all_gather | solution.py:48
  217.6 140.6 %all-gather.11.cloned.1.call-start = ((), (), s32[]{:S(2)}) async-start(), calls=%async_computation.6 | async-start | bytes 8912896 | tf_op jit(solution)/shard_map/all_gather | solution.py:77
  285.2 15.8 %slice-start.8 = ((s8[8388608]{0:T(1024)(128)(4,1)}), s8[4194304]{0:T(1024)(128)(4,1)S(1)}, s32[]{:S(2)}) async-start(s8[8388608]{0:T(1024)(128)(4,1)} %bitcast.373), calls=%async_computation.20 | async-start | bytes 8388608
  291.1 10.0 %copy-start.35 = (bf16[2,2048,512]{2,1,0:T(8,128)(2,1)S(1)}, bf16[2,2048,512]{2,1,0:T(8,128)(2,1)}, u32[]{:S(2)}) copy-start(bf16[2,2048,512]{2,1,0:T(8,128)(2,1)} %param.13) | copy-start | bytes 12582916
  307.0 221.1 %reduce-scatter.6.cloned.1.call-start = ((), (), s32[]{:S(2)}) async-start(), calls=%async_computation.7 | async-start | bytes 17825792 | tf_op jit(solution)/shard_map/reduce_scatter | solution.py:101
  433.1 152.2 %all-gather.13.cloned.1.call-start = ((), (), s32[]{:S(2)}) async-start(), calls=%async_computation.8 | async-start | bytes 8912896 | tf_op jit(solution)/shard_map/all_gather | solution.py:77
  533.0 144.6 %all-gather.17.cloned.1.call-start = ((), (), s32[]{:S(2)}) async-start(), calls=%async_computation.11 | async-start | bytes 8912896 | tf_op jit(solution)/shard_map/all_gather | solution.py:76
  533.8 179.3 %all-gather.15.cloned.1.call-start = ((), (), s32[]{:S(2)}) async-start(), calls=%async_computation.10 | async-start | bytes 8912896 | tf_op jit(solution)/shard_map/all_gather | solution.py:76
  534.6 253.9 %reduce-scatter.8.cloned.1.call-start = ((), (), s32[]{:S(2)}) async-start(), calls=%async_computation.9 | async-start | bytes 17825792 | tf_op jit(solution)/shard_map/reduce_scatter | solution.py:101
  623.8 27.5 %copy-start.6 = (bf16[2048,1,3,128]{0,3,2,1:T(8,128)(2,1)}, bf16[2048,1,3,128]{0,3,2,1:T(8,128)(2,1)S(1)}, u32[]{:S(2)}) copy-start(bf16[2048,1,3,128]{0,3,2,1:T(8,128)(2,1)S(1)} %pad_maximum_fusion.5) | copy-start | bytes 4718596
  677.6 18.9 %slice-start.4 = ((s8[8388608]{0:T(1024)(128)(4,1)}), s8[4194304]{0:T(1024)(128)(4,1)S(1)}, s32[]{:S(2)}) async-start(s8[8388608]{0:T(1024)(128)(4,1)} %bitcast.369), calls=%async_computation.16 | async-start | bytes 8388608
  696.5 14.1 %slice-start = ((s8[8388608]{0:T(1024)(128)(4,1)}), s8[4194304]{0:T(1024)(128)(4,1)S(1)}, s32[]{:S(2)}) async-start(s8[8388608]{0:T(1024)(128)(4,1)} %bitcast.347), calls=%async_computation.12 | async-start | bytes 8388608
  713.1 10.2 %copy-start.42 = (bf16[2048,512]{1,0:T(8,128)(2,1)S(1)}, bf16[2048,512]{1,0:T(8,128)(2,1)}, u32[]{:S(2)}) copy-start(bf16[2048,512]{1,0:T(8,128)(2,1)} %convolution_convert_fusion.13) | copy-start | bytes 6291460
  721.2 14.7 %slice-start.2 = ((s8[8388608]{0:T(1024)(128)(4,1)}), s8[4194304]{0:T(1024)(128)(4,1)S(1)}, s32[]{:S(2)}) async-start(s8[8388608]{0:T(1024)(128)(4,1)} %bitcast.367), calls=%async_computation.14 | async-start | bytes 8388608
  723.4 10.1 %copy-start.15 = (bf16[1,512,2048]{2,1,0:T(8,128)(2,1)S(1)}, bf16[1,512,2048]{2,1,0:T(8,128)(2,1)}, u32[]{:S(2)}) copy-start(bf16[1,512,2048]{2,1,0:T(8,128)(2,1)} %fusion.58) | copy-start | bytes 6291460
  723.4 12.5 %slice-start.3 = ((s8[8388608]{0:T(1024)(128)(4,1)}), s8[4194304]{0:T(1024)(128)(4,1)S(1)}, s32[]{:S(2)}) async-start(s8[8388608]{0:T(1024)(128)(4,1)} %bitcast.367), calls=%async_computation.15 | async-start | bytes 8388608
  747.7 40.8 %copy-start.27 = (f32[1,2048]{1,0:T(1,128)S(1)}, f32[1,2048]{1,0:T(1,128)}, u32[]{:S(2)}) copy-start(f32[1,2048]{1,0:T(1,128)} %copy-done.26) | copy-start | bytes 24580
  747.7 42.4 %copy-start.28 = (f32[2048]{0:T(1024)S(1)}, f32[2048]{0:T(1024)}, u32[]{:S(2)}) copy-start(f32[2048]{0:T(1024)} %get-tuple-element.49) | copy-start | bytes 24580
  747.7 86.2 %copy-start.8 = (bf16[128,2048]{1,0:T(8,128)(2,1)S(1)}, bf16[128,2048]{1,0:T(8,128)(2,1)}, u32[]{:S(2)}) copy-start(bf16[128,2048]{1,0:T(8,128)(2,1)} %fusion.142) | copy-start | bytes 1572868
  (46 other events, 288.9 us)
Sparse Core Ops, SparseCore 0:
  11.5 57.5 all-gather.6
  120.2 94.8 reduce-scatter.3
  217.7 52.1 all-gather.8
  307.1 51.0 all-gather.10
  433.2 94.8 reduce-scatter.5
  533.1 52.1 all-gather.12
  586.9 51.0 all-gather.16
  640.2 51.0 all-gather.14
  693.6 94.8 reduce-scatter.7
where the time goes:
time: 854 us; the launch traced here: 843 us
  waiting for transfers between devices  435 us (51%)
  matrix products  287 us (34%)
  other arithmetic  56.1 us (7%)
  blocking collectives  43.8 us (5%)
  between operations  15.2 us (2%)
    reduce_scatter x2, waiting for transfers between devices, block_backward(): lax.psum_scatter(normed_part, 'tp', scatter_dimension=0, tiled=True)  130 us
    all_gather x2, waiting for transfers between devices, block_forward(): u_full = lax.all_gather(u_loc, 'tp', axis=0, tiled=True)  107 us
    all_gather x2, waiting for transfers between devices, block_backward(): dy_full = lax.all_gather(dy_loc, 'tp', axis=0, tiled=True)  101 us
    reduce_scatter x1, waiting for transfers between devices, block_forward(): lax.psum_scatter(block_part, 'tp', scatter_dimension=0, tiled=True)  94.9 us
    psum x1, blocking collectives, device_program(): grad_gain = lax.psum(jnp.stack([item[0] for item in layer_grads]), 'tp')  43.8 us
    dot_general x2, matrix products, block_backward(): jnp.einsum('sc,dc->sd', d_qkv, w_qkv_l, preferred_element_type=jnp.float32)  39.6 us
    dot_general x2, matrix products, block_backward(): jnp.einsum('sf,sd->fd', hidden, dy_full, preferred_element_type=jnp.float32)  19.7 us
    dot_general x2, matrix products, block_forward(): jnp.dot(u_full, w_up_l, preferred_element_type=jnp.float32)  18.7 us
  transfers between devices with their start and end apart: 9, of which 7 were waited for; matrix products, arithmetic and copies ran while one was open for 20% of the time, Pallas kernels for 0%

commit v1 on v0

v1 whole, which is shorter than its diff:
```python
import functools

import jax
import jax.numpy as jnp
from jax import lax
from jax.experimental import pallas as pl
from jax.experimental.pallas import tpu as pltpu
from jax.sharding import PartitionSpec as P

HEAD_DIM = 128
NORM_EPS = 1e-5
ROPE_BASE = 10000.0
MESH = pl.DeviceIdType.MESH
NP = 4
F32 = jnp.float32
BF16 = jnp.bfloat16


def dot_nn(a, b):
    return lax.dot_general(a, b, (((1,), (0,)), ((), ())), preferred_element_type=F32)


def dot_nt(a, b):
    return lax.dot_general(a, b, (((1,), (1,)), ((), ())), preferred_element_type=F32)


def dot_tn(a, b):
    return lax.dot_general(a, b, (((0,), (0,)), ((), ())), preferred_element_type=F32)


def aligned(index, size):
    return pl.multiple_of(index, size)


class Place:
    def __init__(self, tp_size):
        index = lax.axis_index('tp')
        self.ring = tp_size // 2
        self.half = self.ring // 2
        self.core = lax.rem(index, 2)
        self.chip = lax.div(index, 2)
        self.right = {'tp': self.near(1) * 2 + self.core}
        self.left = {'tp': self.near(-1) * 2 + self.core}
        self.mate = {'tp': self.chip * 2 + 1 - self.core}

    def near(self, step):
        return lax.rem(self.chip + step + self.ring, self.ring)

    def barrier(self, others=()):
        sem = pltpu.get_barrier_semaphore()
        peers = [self.right, self.left, self.mate] + list(others)
        for peer in peers:
            pl.semaphore_signal(sem, inc=1, device_id=peer, device_id_type=MESH)
        pl.semaphore_wait(sem, len(peers))


class Gather:
    def __init__(self, place, buf, shard_rows, sems):
        self.place, self.buf, self.shard = place, buf, shard_rows
        self.rows = shard_rows // NP
        self.events = (place.half - 1) * NP + NP // 2
        self.send_r, self.recv_r, self.send_l, self.recv_l, self.send_m, self.recv_m = sems

    @staticmethod
    def scratch(half):
        events = (half - 1) * NP + NP // 2
        return [pltpu.SemaphoreType.DMA((n,)) for n in (events, events, events, events, 2 * events + NP, 2 * events + NP)]

    def view(self, chip, core, piece):
        start = (chip * 2 + core) * self.shard + piece * self.rows
        return self.buf.at[pl.ds(aligned(start, self.rows), self.rows)]

    def own_rows(self):
        start = (self.place.chip * 2 + self.place.core) * self.shard
        return pl.ds(aligned(start, self.shard), self.shard)

    def to_right(self, event, view):
        return pltpu.make_async_remote_copy(view, view, self.send_r.at[event], self.recv_r.at[event], self.place.right, MESH)

    def to_left(self, event, view):
        return pltpu.make_async_remote_copy(view, view, self.send_l.at[event], self.recv_l.at[event], self.place.left, MESH)

    def to_mate(self, slot, view):
        return pltpu.make_async_remote_copy(view, view, self.send_m.at[slot], self.recv_m.at[slot], self.place.mate, MESH)

    def start(self):
        place = self.place
        for piece in range(NP):
            self.to_right(piece, self.view(place.chip, place.core, piece)).start()
            self.to_left(piece, self.view(place.chip, place.core, NP - 1 - piece)).start()
        for piece in range(NP):
            self.to_mate(2 * self.events + piece, self.view(place.chip, place.core, piece)).start()

    def views(self, event):
        step = lax.div(event, NP) + 1
        piece = lax.rem(event, NP)
        from_left = self.view(self.place.near(-step), self.place.core, piece)
        from_right = self.view(self.place.near(step), self.place.core, NP - 1 - piece)
        return from_left, from_right

    def event(self, event, forward=None):
        from_left, from_right = self.views(event)
        self.to_right(event, from_left).wait_recv()
        self.pass_on(event, forward, lambda: self.to_right(event + NP, from_left).start())
        self.to_mate(event, from_left).start()
        self.to_left(event, from_right).wait_recv()
        self.pass_on(event, forward, lambda: self.to_left(event + NP, from_right).start())
        self.to_mate(self.events + event, from_right).start()

    def pass_on(self, event, forward, send):
        if forward is None:
            pl.when(event + NP < self.events)(send)
        elif forward:
            send()

    def mate_wait(self, first, count):
        for offset in range(count):
            self.to_mate(first + offset, self.view(self.place.chip, 1 - self.place.core, 0)).wait_recv()

    def mate_wait_all(self):
        def body(slot, carry):
            self.mate_wait(slot, 1)
            return carry
        lax.fori_loop(0, 2 * self.events + NP, body, 0)

    def mate_wait_last(self):
        first = (self.place.half - 1) * NP
        self.mate_wait(first, NP // 2)
        self.mate_wait(self.events + first, NP // 2)

    def mate_wait_chip(self, distance, rightward):
        ring_first = lax.select(rightward, self.events, 0) + (distance - 1) * NP
        self.mate_wait(lax.select(distance == 0, 2 * self.events, ring_first), NP)

    def finish(self):
        view = self.view(self.place.chip, self.place.core, 0)

        def ring(event, carry):
            self.to_right(event, view).wait_send()
            self.to_left(event, view).wait_send()
            return carry
        lax.fori_loop(0, self.events, ring, 0)

        def across(slot, carry):
            self.to_mate(slot, view).wait_send()
            return carry
        lax.fori_loop(0, 2 * self.events + NP, across, 0)


class Reduce:
    def __init__(self, place, part, shard_rows, refs):
        self.place, self.part, self.shard = place, part, shard_rows
        self.events = (place.half - 1) * NP + NP // 2
        self.ring_r, self.ring_l, self.acc, self.stage = refs[:4]
        self.send_r, self.recv_r, self.send_l, self.recv_l, self.send_m, self.recv_m = refs[4:]

    @staticmethod
    def scratch(half, shard_rows, width):
        events = (half - 1) * NP + NP // 2
        shapes = [(events,), (events,), (2 * events + NP,), (6, 2)]
        sems = (events, events, events, events, 2 * events + NP, 2 * events + NP)
        return [pltpu.VMEM(s + (shard_rows, width), F32) for s in shapes] + [pltpu.SemaphoreType.DMA((n,)) for n in sems]

    def slot(self, event, way):
        return lax.rem(event, 2) * 2 + way

    def mate_copy(self, slot, index):
        return pltpu.make_async_remote_copy(
            self.stage.at[slot, 1 - self.place.core], self.acc.at[index], self.send_m.at[index], self.recv_m.at[index],
            self.place.mate, MESH)

    def ring_copy(self, event, way):
        if way == 0:
            return pltpu.make_async_remote_copy(
                self.acc.at[2 * event], self.ring_r.at[event], self.send_r.at[event], self.recv_r.at[event], self.place.right, MESH)
        return pltpu.make_async_remote_copy(
            self.acc.at[2 * event + 1], self.ring_l.at[event], self.send_l.at[event], self.recv_l.at[event], self.place.left, MESH)

    def fill(self, chip, piece, slot, index):
        value = self.part(chip, piece)
        self.stage[slot, 0] = value[:self.shard]
        self.stage[slot, 1] = value[self.shard:]
        self.mate_copy(slot, index).start()

    def prepare(self, event, reuse=True):
        shifted = event + NP // 2
        distance = self.place.half - lax.div(shifted, NP)
        piece = lax.rem(shifted, NP)
        for way in range(2):
            slot = self.slot(event, way)
            if reuse:
                self.mate_copy(slot, 2 * (event - 2) + way).wait_send()
            if way == 0:
                self.fill(self.place.near(distance), piece, slot, 2 * event)
            else:
                self.fill(self.place.near(-distance), NP - 1 - piece, slot, 2 * event + 1)

    def prepare_own(self, second):
        event = self.events + (1 if second else 0)
        for way in range(2):
            slot = 4 + way if second else self.slot(self.events, way)
            if not second:
                self.mate_copy(slot, 2 * (event - 2) + way).wait_send()
            self.fill(self.place.chip, (2 if second else 0) + way, slot, 2 * event + way)

    def event(self, event, arrives):
        for way in range(2):
            index = 2 * event + way
            slot = self.slot(event, way)
            self.mate_copy(slot, index).wait_recv()
            total = self.stage[slot, self.place.core] + self.acc[index]
            if arrives:
                self.ring_copy(event - NP, way).wait_recv()
                ring = self.ring_r if way == 0 else self.ring_l
                total = total + ring[event - NP]
            self.acc[index] = total
            self.ring_copy(event, way).start()

    def final(self, piece):
        last = self.events - NP
        index = 2 * self.events + piece
        slot = piece % 2 + (4 if piece >= 2 else 2 * (self.events % 2))
        self.mate_copy(slot, index).wait_recv()
        self.ring_copy(last + piece, 0).wait_recv()
        self.ring_copy(last + NP - 1 - piece, 1).wait_recv()
        return ((self.stage[slot, self.place.core] + self.acc[index])
                + (self.ring_r[last + piece] + self.ring_l[last + NP - 1 - piece]))

    def final_order(self):
        return range(NP)

    def finish(self):
        for event in range(self.events - 1, self.events + 2):
            for way in range(2):
                self.mate_copy(0, 2 * event + way).wait_send()

        def ring(event, carry):
            self.ring_copy(event, 0).wait_send()
            self.ring_copy(event, 1).wait_send()
            return carry
        lax.fori_loop(0, self.events, ring, 0)

    def run(self, filler):
        self.prepare(0, reuse=False)

        def first(event, carry):
            self.event(event, False)

            @pl.when(event < 1)
            def _():
                self.prepare(event + 1, reuse=False)

            @pl.when(event >= 1)
            def _():
                self.prepare(event + 1)
            filler(event)
            return carry

        def later(event, carry):
            self.event(event, True)

            @pl.when(event + 1 < self.events)
            def _():
                self.prepare(event + 1)

            @pl.when(event + 1 == self.events)
            def _():
                self.prepare_own(False)

            @pl.when(event == NP)
            def _():
                self.prepare_own(True)
            filler(event)
            return carry
        lax.fori_loop(0, NP, first, 0)
        lax.fori_loop(NP, self.events, later, 0)


def rope_pair(table):
    lanes = lax.broadcasted_iota(jnp.int32, table.shape, 1)
    swapped = pltpu.roll(table, HEAD_DIM // 2, 1)
    low = lanes < HEAD_DIM // 2
    return jnp.where(low, table, swapped), jnp.where(low, -swapped, table)


def rope(values, table, inverse=False):
    cos2, sin2 = rope_pair(table)
    turned = pltpu.roll(values, HEAD_DIM // 2, 1)
    if inverse:
        return values * cos2 - turned * sin2
    return values * cos2 + turned * sin2


def norm_forward(x_f32, gain_row):
    inv = lax.rsqrt(jnp.mean(x_f32 * x_f32, axis=-1, keepdims=True) + NORM_EPS)
    return (x_f32 * inv * gain_row).astype(BF16)


def norm_backward(x_f32, gain_row, d_normed):
    inv = lax.rsqrt(jnp.mean(x_f32 * x_f32, axis=-1, keepdims=True) + NORM_EPS)
    unit = x_f32 * inv
    d_unit = d_normed * gain_row
    d_x = inv * (d_unit - unit * jnp.mean(d_unit * unit, axis=-1, keepdims=True))
    return d_x, jnp.sum(d_normed * unit, axis=0, keepdims=True)


def attention_block(row0, rows, keys, refs, forward, backward):
    q_ref, k_ref, v_ref, table_ref, read_da, write_o, dx_ref, dk_ref, dv_ref = refs
    here = pl.ds(aligned(row0, rows), rows)
    scale = HEAD_DIM ** -0.5
    query = q_ref[here]
    scores = dot_nt(query, k_ref[0:keys]) * scale
    row_id = row0 + lax.broadcasted_iota(jnp.int32, scores.shape, 0)
    col_id = lax.broadcasted_iota(jnp.int32, scores.shape, 1)
    scores = jnp.where(row_id >= col_id, scores, -1e30)
    expd = jnp.exp(scores - jnp.max(scores, axis=-1, keepdims=True))
    prob = expd * (1.0 / jnp.sum(expd, axis=-1, keepdims=True))
    prob_b = prob.astype(BF16)
    d_attn = read_da(here) if backward else None
    if forward:
        write_o(here, dot_nn(prob_b, v_ref[0:keys]).astype(BF16))
    if backward:
        dv_ref[0:keys] += dot_tn(prob_b, d_attn)
        d_prob = dot_nt(d_attn, v_ref[0:keys]).astype(BF16).astype(F32)
        row_dot = jnp.sum(prob * d_prob, axis=-1, keepdims=True)
        d_scores = (prob * (d_prob - row_dot) * scale).astype(BF16)
        d_query = dot_nn(d_scores, k_ref[0:keys]).astype(BF16).astype(F32)
        dx_ref[here, 0:HEAD_DIM] = rope(d_query, table_ref[here], inverse=True).astype(BF16)
        dk_ref[0:keys] += dot_tn(d_scores, query)


def store_keys_values(dx_ref, dk_ref, dv_ref, table_ref, rows):
    def body(block, carry):
        here = pl.ds(aligned(block * rows, rows), rows)
        d_key = dk_ref[here].astype(BF16).astype(F32)
        dx_ref[here, HEAD_DIM:2 * HEAD_DIM] = rope(d_key, table_ref[here], inverse=True).astype(BF16)
        dx_ref[here, 2 * HEAD_DIM:3 * HEAD_DIM] = dv_ref[here].astype(BF16)
        return carry
    lax.fori_loop(0, dx_ref.shape[0] // rows, body, 0)


def gated_pull(gate, up, d_hidden):
    sig = jax.nn.sigmoid(gate)
    silu = gate * sig
    d_silu = d_hidden * up
    return (silu * up).astype(BF16), (d_silu * sig + d_silu * silu * (1.0 - sig)).astype(BF16), (d_hidden * silu).astype(BF16)


class Copies:
    def __init__(self, sems):
        self.sems, self.used = sems, 0

    def start(self, src, dst):
        copy = pltpu.make_async_copy(src, dst, self.sems.at[self.used])
        self.used += 1
        copy.start()
        return copy


def gather_units(gather, unit, event):
    step = lax.div(event, NP) + 1
    piece = lax.rem(event, NP)
    last = gather.events - 1
    own = event == 1
    near = (event >= NP) & (lax.rem(event, 2) == 0)
    final = event == last

    @pl.when(own | near | final)
    def _():
        distance = step - 1
        rightward = final | (piece != 0)
        gather.mate_wait_chip(distance, rightward)
        chip = gather.place.near(lax.select(rightward, distance, -distance))
        unit(chip)


def kernel_first(tp_size, x_ref, gain_ref, gy_hbm, table_hbm, wqkv_hbm, wout_hbm, wgate_hbm, wup_hbm, wdown_hbm,
                 x1_out, u1_out, u0_out, gy_out, q_out, k_out, v_out, o_out, ab_out, dah_out, *scratch):
    n_gather, n_reduce = 6, 10
    (u_ref, g_ref, wc_ref, wo_ref, wo1_ref, q_ref, k_ref, v_ref, om_ref, ab_ref, dah_ref, table_ref, y_ref, local) = scratch[:14]
    sems_u = scratch[14:14 + n_gather]
    sems_g = scratch[14 + n_gather:14 + 2 * n_gather]
    refs_r = scratch[14 + 2 * n_gather:]
    place = Place(tp_size)
    shard, width = x_ref.shape
    pair = 2 * shard
    chips = place.ring
    head_cols = wqkv_hbm.shape[2]
    ff = wgate_hbm.shape[2]
    piece_cols = width // NP

    loads = Copies(local)
    gu = Gather(place, u_ref, shard, sems_u)
    gg = Gather(place, g_ref, shard, sems_g)
    load_g = loads.start(gy_hbm, g_ref.at[gg.own_rows()])
    load_w = [loads.start(wqkv_hbm.at[0], wc_ref.at[:, 0:head_cols]),
              loads.start(wgate_hbm.at[0], wc_ref.at[:, head_cols:head_cols + ff]),
              loads.start(wup_hbm.at[0], wc_ref.at[:, head_cols + ff:head_cols + 2 * ff]),
              loads.start(table_hbm, table_ref)]
    load_o = []
    for piece in range(NP):
        cols = slice(piece * piece_cols, (piece + 1) * piece_cols)
        load_o.append(loads.start(wout_hbm.at[0, :, cols], wo_ref.at[piece, 0:HEAD_DIM]))
        load_o.append(loads.start(wdown_hbm.at[0, :, cols], wo_ref.at[piece, HEAD_DIM:HEAD_DIM + ff]))
    load_o.append(loads.start(wout_hbm.at[1], wo1_ref.at[0:HEAD_DIM]))
    load_o.append(loads.start(wdown_hbm.at[1], wo1_ref.at[HEAD_DIM:HEAD_DIM + ff]))

    x_f32 = x_ref[...].astype(F32)
    u_own = norm_forward(x_f32, gain_ref[0:1])
    u_ref[gu.own_rows()] = u_own
    u0_out[...] = u_own
    place.barrier()
    gu.start()
    load_g.wait()
    for copy in load_w:
        copy.wait()

    n_out = loads.used

    def ab_copy(slot, here):
        return pltpu.make_async_copy(ab_ref.at[slot], ab_out.at[here], local.at[n_out + slot])

    def unit(count, chip):
        here = pl.ds(aligned(chip * pair, pair), pair)
        slot = lax.rem(count, 2)
        rows_u = u_ref[here]
        qkv = dot_nn(rows_u, wc_ref[:, 0:head_cols]).astype(BF16)
        table = table_ref[here]
        q_ref[here] = rope(qkv[:, 0:HEAD_DIM].astype(F32), table).astype(BF16)
        k_ref[here] = rope(qkv[:, HEAD_DIM:2 * HEAD_DIM].astype(F32), table).astype(BF16)
        v_ref[here] = qkv[:, 2 * HEAD_DIM:3 * HEAD_DIM]

        @pl.when(count >= 2)
        def _():
            ab_copy(slot, here).wait()
        gate = dot_nn(rows_u, wc_ref[:, head_cols:head_cols + ff]).astype(BF16)
        up = dot_nn(rows_u, wc_ref[:, head_cols + ff:head_cols + 2 * ff]).astype(BF16)
        ab_ref[slot, :, 0:ff] = gate
        ab_ref[slot, :, ff:2 * ff] = up
        gate_f, up_f = gate.astype(F32), up.astype(F32)
        om_ref[here, HEAD_DIM:HEAD_DIM + ff] = (gate_f * jax.nn.sigmoid(gate_f) * up_f).astype(BF16)
        ab_copy(slot, here).start()

    def unit_count(event):
        return lax.select(event == 1, 0, lax.select(event == gu.events - 1, chips - 2, lax.div(event, 2) - 1))

    def loop_u(event, carry):
        gu.event(event)

        @pl.when(event == gu.events - NP)
        def _():
            gg.start()
        gather_units(gu, functools.partial(unit, unit_count(event)), event)
        return carry
    lax.fori_loop(0, gu.events, loop_u, 0)
    gu.mate_wait_last()
    unit(jnp.int32(chips - 1), place.near(place.half))

    def write_o(here, value):
        om_ref[here, 0:HEAD_DIM] = value

    blocks = chips
    refs_a = (q_ref, k_ref, v_ref, table_ref, None, write_o, None, None, None)

    def loop_g(event, carry):
        gg.event(event, forward=True)

        @pl.when(event < blocks)
        def _():
            attention_block(event * pair, pair, chips * pair, refs_a, True, False)
        return carry
    lax.fori_loop(0, gg.events - NP, loop_g, 0)
    for copy in load_o:
        copy.wait()

    outs = Copies(local)
    outs.used = n_out + 2
    saves = [outs.start(q_ref, q_out), outs.start(k_ref, k_out), outs.start(v_ref, v_out),
             outs.start(om_ref.at[:, 0:HEAD_DIM], o_out)]
    n_dah = outs.used + 1

    def gy_copy():
        return pltpu.make_async_copy(g_ref, gy_out, local.at[n_dah - 1])

    def dah_copy(slot, here):
        return pltpu.make_async_copy(dah_ref.at[slot], dah_out.at[here], local.at[n_dah + slot])

    def part(chip, piece):
        here = pl.ds(aligned(chip * pair, pair), pair)
        return dot_nn(om_ref[here], wo_ref[piece])

    reduce = Reduce(place, part, shard, refs_r)

    def filler(event):
        @pl.when(event < NP)
        def _():
            gg.event(gg.events - NP + event, forward=False)

        @pl.when(event == NP - 1)
        def _():
            gg.mate_wait_all()
            gy_copy().start()

        @pl.when((event >= NP) & (event < NP + chips))
        def _():
            block = event - NP
            here = pl.ds(aligned(block * pair, pair), pair)
            slot = lax.rem(block, 2)

            @pl.when(block >= 2)
            def _():
                dah_copy(slot, here).wait()
            dah_ref[slot] = dot_nt(g_ref[here], wo1_ref[...]).astype(BF16)
            dah_copy(slot, here).start()

    reduce.run(filler)
    for piece in reduce.final_order():
        y_ref[:, piece * piece_cols:(piece + 1) * piece_cols] = reduce.final(piece)
    x_next = (x_ref[...].astype(F32) + y_ref[...]).astype(BF16)
    x1_out[...] = x_next
    u1_out[...] = norm_forward(x_next.astype(F32), gain_ref[1:2])
    gu.finish()
    gg.finish()
    reduce.finish()
    for copy in saves:
        copy.wait()
    gy_copy().wait()
    for slot in range(2):
        ab_copy(slot, pl.ds(0, pair)).wait()
        dah_copy(slot, pl.ds(0, pair)).wait()


def weight_grads_u(block, u_ref, dx_ref, stage_ref, outs, sems, head_cols, ff):
    rows = stage_ref.shape[1]
    slot = lax.rem(block, 2)
    here = pl.ds(aligned(block * rows, rows), rows)

    def copies():
        bounds = (0, head_cols, head_cols + ff, head_cols + 2 * ff)
        return [pltpu.make_async_copy(stage_ref.at[slot, :, bounds[i]:bounds[i + 1]], outs[i].at[here], sems.at[slot, i]) for i in range(3)]

    @pl.when(block >= 2)
    def _():
        for copy in copies():
            copy.wait()
    stage_ref[slot] = dot_tn(u_ref[:, here], dx_ref[...]).astype(BF16)
    for copy in copies():
        copy.start()


def weight_grads_u_wait(stage_ref, outs, sems, head_cols, ff):
    rows = stage_ref.shape[1]
    bounds = (0, head_cols, head_cols + ff, head_cols + 2 * ff)
    for slot in range(2):
        for i in range(3):
            pltpu.make_async_copy(stage_ref.at[slot, :, bounds[i]:bounds[i + 1]], outs[i].at[pl.ds(0, rows)], sems.at[slot, i]).wait()


def weight_grads_h(piece, ho_ref, read_dy, stage_ref, outs, sems, ff):
    cols = stage_ref.shape[2]
    stage_ref[piece] = dot_tn(ho_ref[...], read_dy(piece)).astype(BF16)
    for copy in h_copies(piece, stage_ref, outs, sems, ff):
        copy.start()


def h_copies(piece, stage_ref, outs, sems, ff):
    cols = stage_ref.shape[2]
    there = pl.ds(aligned(piece * cols, cols), cols)
    return [pltpu.make_async_copy(stage_ref.at[piece, 0:HEAD_DIM], outs[0].at[:, there], sems.at[piece, 0]),
            pltpu.make_async_copy(stage_ref.at[piece, HEAD_DIM:HEAD_DIM + ff], outs[1].at[:, there], sems.at[piece, 1])]


def kernel_last_block(tp_size, x_ref, dy_ref, gain_ref, u_hbm, gy_hbm, dah_hbm, table_hbm, wqkv_hbm, wgate_hbm, wup_hbm,
                      dx_out, gain_out, gqkv_out, gout_out, ggate_out, gup_out, gdown_out, *scratch):
    n_gather = 6
    (u_ref, wc_ref, dx_ref, ho_ref, gy_ref, q_ref, k_ref, v_ref, dk_ref, dv_ref, table_ref, y_ref, gs_ref, hs_ref, local,
     sems_gs, sems_hs, sems_gy) = scratch[:18]
    sems_u = scratch[18:18 + n_gather]
    refs_r = scratch[18 + n_gather:]
    place = Place(tp_size)
    shard, width = x_ref.shape
    pair = 2 * shard
    chips = place.ring
    head_cols = wqkv_hbm.shape[2]
    ff = wgate_hbm.shape[2]
    piece_cols = width // NP

    loads = Copies(local)
    gu = Gather(place, u_ref, shard, sems_u)
    load_u = loads.start(u_hbm, u_ref.at[gu.own_rows()])
    load_w = [loads.start(wqkv_hbm.at[1], wc_ref.at[:, 0:head_cols]),
              loads.start(wgate_hbm.at[1], wc_ref.at[:, head_cols:head_cols + ff]),
              loads.start(wup_hbm.at[1], wc_ref.at[:, head_cols + ff:head_cols + 2 * ff]),
              loads.start(table_hbm, table_ref),
              loads.start(dah_hbm, ho_ref)]

    def gy_load(piece):
        slot = piece % 2 if isinstance(piece, int) else lax.rem(piece, 2)
        cols = pl.ds(aligned(piece * piece_cols, piece_cols), piece_cols)
        return pltpu.make_async_copy(gy_hbm.at[:, cols], gy_ref.at[slot], sems_gy.at[slot])

    gy_load(0).start()
    gy_load(1).start()
    place.barrier()
    load_u.wait()
    gu.start()
    dk_ref[...] = jnp.zeros_like(dk_ref)
    dv_ref[...] = jnp.zeros_like(dv_ref)
    for copy in load_w:
        copy.wait()

    def unit(chip):
        here = pl.ds(aligned(chip * pair, pair), pair)
        rows_u = u_ref[here]
        qkv = dot_nn(rows_u, wc_ref[:, 0:head_cols]).astype(BF16)
        table = table_ref[here]
        q_ref[here] = rope(qkv[:, 0:HEAD_DIM].astype(F32), table).astype(BF16)
        k_ref[here] = rope(qkv[:, HEAD_DIM:2 * HEAD_DIM].astype(F32), table).astype(BF16)
        v_ref[here] = qkv[:, 2 * HEAD_DIM:3 * HEAD_DIM]
        gate = dot_nn(rows_u, wc_ref[:, head_cols:head_cols + ff]).astype(BF16).astype(F32)
        up = dot_nn(rows_u, wc_ref[:, head_cols + ff:head_cols + 2 * ff]).astype(BF16).astype(F32)
        d_hidden = ho_ref[here, HEAD_DIM:HEAD_DIM + ff].astype(F32)
        hidden, d_gate, d_up = gated_pull(gate, up, d_hidden)
        ho_ref[here, HEAD_DIM:HEAD_DIM + ff] = hidden
        dx_ref[here, head_cols:head_cols + ff] = d_gate
        dx_ref[here, head_cols + ff:head_cols + 2 * ff] = d_up

    def loop_u(event, carry):
        gu.event(event)
        gather_units(gu, unit, event)
        return carry
    lax.fori_loop(0, gu.events, loop_u, 0)
    gu.mate_wait_last()
    unit(place.near(place.half))

    def read_da(here):
        return ho_ref[here, 0:HEAD_DIM]

    def write_o(here, value):
        ho_ref[here, 0:HEAD_DIM] = value

    refs_a = (q_ref, k_ref, v_ref, table_ref, read_da, write_o, dx_ref, dk_ref, dv_ref)
    groups = 4
    for group in range(groups):
        def body(block, carry, group=group):
            attention_block(block * pair, pair, (group + 1) * (chips * pair // groups), refs_a, True, True)
            return carry
        lax.fori_loop(group * chips // groups, (group + 1) * chips // groups, body, 0)
    store_keys_values(dx_ref, dk_ref, dv_ref, table_ref, pair)

    def part(chip, piece):
        here = pl.ds(aligned(chip * pair, pair), pair)
        return dot_nt(dx_ref[here], wc_ref[pl.ds(aligned(piece * piece_cols, piece_cols), piece_cols)])

    reduce = Reduce(place, part, shard, refs_r)
    outs_u = (gqkv_out, ggate_out, gup_out)
    outs_h = (gout_out, gdown_out)

    def read_dy(piece):
        return gy_ref[lax.rem(piece, 2)]

    def filler(event):
        @pl.when(event < NP)
        def _():
            gy_load(event).wait()
            weight_grads_h(event, ho_ref, read_dy, hs_ref, outs_h, sems_hs, ff)

            @pl.when(event + 2 < NP)
            def _():
                gy_load(event + 2).start()

        @pl.when((event >= NP) & (event < NP + chips))
        def _():
            weight_grads_u(event - NP, u_ref, dx_ref, gs_ref, outs_u, sems_gs, head_cols, ff)

    reduce.run(filler)
    for piece in reduce.final_order():
        y_ref[:, piece * piece_cols:(piece + 1) * piece_cols] = reduce.final(piece)
    d_normed = y_ref[...].astype(BF16).astype(F32)
    d_x, gain_part = norm_backward(x_ref[...].astype(F32), gain_ref[1:2], d_normed)
    dx_out[...] = (dy_ref[...].astype(F32) + d_x).astype(BF16)
    gain_out[...] = gain_part
    gu.finish()
    reduce.finish()
    for piece in range(NP):
        for copy in h_copies(piece, hs_ref, outs_h, sems_hs, ff):
            copy.wait()
    weight_grads_u_wait(gs_ref, outs_u, sems_gs, head_cols, ff)


def kernel_first_block(tp_size, x_ref, dy_ref, gain_ref, gain1_ref, u_hbm, q_hbm, k_hbm, v_hbm, o_hbm, ab_hbm, table_hbm,
                       wqkv_hbm, wout_hbm, wgate_hbm, wup_hbm, wdown_hbm,
                       dx_out, gain_out, gqkv_out, gout_out, ggate_out, gup_out, gdown_out, *scratch):
    n_gather = 6
    (u_ref, g_ref, wc_ref, dx_ref, ho_ref, q_ref, k_ref, v_ref, dk_ref, dv_ref, table_ref, y_ref, gs_ref, hs_ref,
     pair_ref, all_ref, local, sems_gs, sems_hs, sem_ps, sem_pr, sem_as, sem_ar) = scratch[:23]
    sems_u = scratch[23:23 + n_gather]
    sems_g = scratch[23 + n_gather:23 + 2 * n_gather]
    refs_r = scratch[23 + 2 * n_gather:]
    place = Place(tp_size)
    shard, width = x_ref.shape
    pair = 2 * shard
    chips = place.ring
    head_cols = wqkv_hbm.shape[2]
    ff = wgate_hbm.shape[2]
    piece_cols = width // NP

    loads = Copies(local)
    gu = Gather(place, u_ref, shard, sems_u)
    gg = Gather(place, g_ref, shard, sems_g)
    load_u = loads.start(u_hbm, u_ref.at[gu.own_rows()])
    load_h = []
    for piece in range(NP):
        cols = slice(piece * piece_cols, (piece + 1) * piece_cols)
        load_h.append(loads.start(wout_hbm.at[0, :, cols], hs_ref.at[piece, 0:HEAD_DIM]))
        load_h.append(loads.start(wdown_hbm.at[0, :, cols], hs_ref.at[piece, HEAD_DIM:HEAD_DIM + ff]))
    load_h.append(loads.start(ab_hbm, dx_ref.at[:, head_cols:head_cols + 2 * ff]))
    load_a = [loads.start(q_hbm, q_ref), loads.start(k_hbm, k_ref), loads.start(v_hbm, v_ref),
              loads.start(o_hbm, ho_ref.at[:, 0:HEAD_DIM]),
              loads.start(table_hbm, table_ref),
              loads.start(wqkv_hbm.at[0], wc_ref.at[:, 0:head_cols]),
              loads.start(wgate_hbm.at[0], wc_ref.at[:, head_cols:head_cols + ff]),
              loads.start(wup_hbm.at[0], wc_ref.at[:, head_cols + ff:head_cols + 2 * ff])]

    g_ref[gg.own_rows()] = dy_ref[...]
    others = [{'tp': place.near(step) * 2 + place.core} for step in range(2, chips - 1)]
    place.barrier(others)
    gg.start()
    dk_ref[...] = jnp.zeros_like(dk_ref)
    dv_ref[...] = jnp.zeros_like(dv_ref)
    load_u.wait()
    for copy in load_h:
        copy.wait()

    def unit(chip):
        here = pl.ds(aligned(chip * pair, pair), pair)
        dah = dot_nt(g_ref[here, 0:piece_cols], hs_ref[0])
        for piece in range(1, NP):
            dah = dah + dot_nt(g_ref[here, piece * piece_cols:(piece + 1) * piece_cols], hs_ref[piece])
        dx_ref[here, 0:HEAD_DIM] = dah[:, 0:HEAD_DIM].astype(BF16)
        d_hidden = dah[:, HEAD_DIM:HEAD_DIM + ff].astype(BF16).astype(F32)
        gate = dx_ref[here, head_cols:head_cols + ff].astype(F32)
        up = dx_ref[here, head_cols + ff:head_cols + 2 * ff].astype(F32)
        hidden, d_gate, d_up = gated_pull(gate, up, d_hidden)
        ho_ref[here, HEAD_DIM:HEAD_DIM + ff] = hidden
        dx_ref[here, head_cols:head_cols + ff] = d_gate
        dx_ref[here, head_cols + ff:head_cols + 2 * ff] = d_up

    def loop_g(event, carry):
        gg.event(event)

        @pl.when(event == gg.events - NP)
        def _():
            gu.start()
        gather_units(gg, unit, event)
        return carry
    lax.fori_loop(0, gg.events, loop_g, 0)
    gg.mate_wait_last()
    unit(place.near(place.half))
    for copy in load_a:
        copy.wait()

    def read_da(here):
        return dx_ref[here, 0:HEAD_DIM]

    refs_a = (q_ref, k_ref, v_ref, table_ref, read_da, None, dx_ref, dk_ref, dv_ref)
    step_rows = shard

    def loop_u(event, carry):
        gu.event(event, forward=True)

        @pl.when(event < chips)
        def _():
            def body(sub, inner):
                attention_block((event * 2 + sub) * step_rows, step_rows, chips * pair, refs_a, False, True)
                return inner
            lax.fori_loop(0, 2, body, 0)
        return carry
    lax.fori_loop(0, gu.events - NP, loop_u, 0)
    store_keys_values(dx_ref, dk_ref, dv_ref, table_ref, pair)

    def part(chip, piece):
        here = pl.ds(aligned(chip * pair, pair), pair)
        return dot_nt(dx_ref[here], wc_ref[pl.ds(aligned(piece * piece_cols, piece_cols), piece_cols)])

    reduce = Reduce(place, part, shard, refs_r)
    outs_u = (gqkv_out, ggate_out, gup_out)
    outs_h = (gout_out, gdown_out)

    def read_dy(piece):
        return g_ref[:, pl.ds(aligned(piece * piece_cols, piece_cols), piece_cols)]

    def filler(event):
        @pl.when(event < NP)
        def _():
            gu.event(gu.events - NP + event, forward=False)
            weight_grads_h(event, ho_ref, read_dy, hs_ref, outs_h, sems_hs, ff)

        @pl.when(event == NP - 1)
        def _():
            gu.mate_wait_all()

        @pl.when((event >= NP) & (event < NP + chips))
        def _():
            weight_grads_u(event - NP, u_ref, dx_ref, gs_ref, outs_u, sems_gs, head_cols, ff)

    reduce.run(filler)
    for piece in reduce.final_order():
        y_ref[:, piece * piece_cols:(piece + 1) * piece_cols] = reduce.final(piece)
    d_normed = y_ref[...].astype(BF16).astype(F32)
    d_x, gain_part = norm_backward(x_ref[...].astype(F32), gain_ref[0:1], d_normed)

    lanes = 128
    tiles = width // lanes
    for tile in range(tiles):
        pair_ref[0, tile:tile + 1] = gain_part[:, tile * lanes:(tile + 1) * lanes]
        pair_ref[0, tiles + tile:tiles + tile + 1] = gain1_ref[:, tile * lanes:(tile + 1) * lanes]
    cross = pltpu.make_async_remote_copy(pair_ref.at[0], pair_ref.at[1], sem_ps, sem_pr, place.mate, MESH)
    cross.start()
    dx_out[...] = (dy_ref[...].astype(F32) + d_x).astype(BF16)
    cross.wait()
    all_ref[place.chip] = pair_ref[0] + pair_ref[1]

    def spread(step):
        return pltpu.make_async_remote_copy(
            all_ref.at[place.chip], all_ref.at[place.chip], sem_as.at[step - 1], sem_ar.at[step - 1],
            {'tp': place.near(step) * 2 + place.core}, MESH)
    for step in range(1, chips):
        spread(step).start()
    gu.finish()
    gg.finish()
    reduce.finish()
    for piece in range(NP):
        for copy in h_copies(piece, hs_ref, outs_h, sems_hs, ff):
            copy.wait()
    weight_grads_u_wait(gs_ref, outs_u, sems_gs, head_cols, ff)
    for step in range(1, chips):
        spread(step).wait()
    total = all_ref[0]
    for chip in range(1, chips):
        total = total + all_ref[chip]
    gain_out[...] = total


def solution(mesh):
    tp_size = mesh.shape['tp']
    half = tp_size // 4
    row_spec = P(('dp', 'tp'), None)
    col_spec = P(None, None, 'tp')
    inner_spec = P(None, 'tp', None)

    def device_program(x_loc, dy_loc, norm_gain, w_qkv, w_out, w_gate, w_up, w_down):
        shard, width = x_loc.shape
        seq = shard * tp_size
        pair = 2 * shard
        chips = tp_size // 2
        head_cols = w_qkv.shape[2]
        ff = w_gate.shape[2]
        cols = head_cols + 2 * ff
        piece_cols = width // NP
        vmem, anyspace = pl.BlockSpec(memory_space=pltpu.VMEM), pl.BlockSpec(memory_space=pl.ANY)
        shape = jax.ShapeDtypeStruct
        dma = pltpu.SemaphoreType.DMA

        half_dim = HEAD_DIM // 2
        freqs = ROPE_BASE ** (-2.0 * jnp.arange(half_dim, dtype=F32) / HEAD_DIM)
        angles = jnp.arange(seq, dtype=F32)[:, None] * freqs[None, :]
        table = jnp.concatenate([jnp.cos(angles), jnp.sin(angles)], axis=1)

        def params(number):
            return pltpu.CompilerParams(collective_id=number, has_side_effects=True, vmem_limit_bytes=67043328)

        rows_shape = shape((shard, width), BF16)
        head_shape = shape((seq, HEAD_DIM), BF16)
        gathers = Gather.scratch(half)
        reduces = Reduce.scratch(half, shard, piece_cols)
        x1, u1, u0, gy_full, q0, k0, v0, o0, ab0, dah1 = pl.pallas_call(
            functools.partial(kernel_first, tp_size),
            out_shape=(rows_shape, rows_shape, rows_shape, shape((seq, width), BF16), head_shape, head_shape, head_shape, head_shape,
                       shape((seq, 2 * ff), BF16), shape((seq, HEAD_DIM + ff), BF16)),
            in_specs=[vmem, vmem] + [anyspace] * 7,
            out_specs=(vmem, vmem, vmem) + (anyspace,) * 7,
            scratch_shapes=[
                pltpu.VMEM((seq, width), BF16), pltpu.VMEM((seq, width), BF16), pltpu.VMEM((width, cols), BF16),
                pltpu.VMEM((NP, HEAD_DIM + ff, piece_cols), BF16), pltpu.VMEM((HEAD_DIM + ff, width), BF16),
                pltpu.VMEM((seq, HEAD_DIM), BF16), pltpu.VMEM((seq, HEAD_DIM), BF16), pltpu.VMEM((seq, HEAD_DIM), BF16),
                pltpu.VMEM((seq, HEAD_DIM + ff), BF16), pltpu.VMEM((2, pair, 2 * ff), BF16), pltpu.VMEM((2, pair, HEAD_DIM + ff), BF16),
                pltpu.VMEM((seq, HEAD_DIM), F32), pltpu.VMEM((shard, width), F32), dma((32,))] + gathers + gathers + reduces,
            compiler_params=params(1), name='first_forward',
        )(x_loc, norm_gain, dy_loc, table, w_qkv, w_out, w_gate, w_up, w_down)

        grad_shapes = (rows_shape, shape((1, width), F32), shape((width, head_cols), BF16), shape((HEAD_DIM, width), BF16),
                       shape((width, ff), BF16), shape((width, ff), BF16), shape((ff, width), BF16))
        dx1, gain1, gqkv1, gout1, ggate1, gup1, gdown1 = pl.pallas_call(
            functools.partial(kernel_last_block, tp_size),
            out_shape=grad_shapes,
            in_specs=[vmem, vmem, vmem] + [anyspace] * 7,
            out_specs=(vmem, vmem) + (anyspace,) * 5,
            scratch_shapes=[
                pltpu.VMEM((seq, width), BF16), pltpu.VMEM((width, cols), BF16), pltpu.VMEM((seq, cols), BF16),
                pltpu.VMEM((seq, HEAD_DIM + ff), BF16), pltpu.VMEM((2, seq, piece_cols), BF16),
                pltpu.VMEM((seq, HEAD_DIM), BF16), pltpu.VMEM((seq, HEAD_DIM), BF16), pltpu.VMEM((seq, HEAD_DIM), BF16),
                pltpu.VMEM((seq, HEAD_DIM), F32), pltpu.VMEM((seq, HEAD_DIM), F32), pltpu.VMEM((seq, HEAD_DIM), F32),
                pltpu.VMEM((shard, width), F32), pltpu.VMEM((2, width // chips, cols), BF16),
                pltpu.VMEM((NP, HEAD_DIM + ff, piece_cols), BF16),
                dma((16,)), dma((2, 3)), dma((NP, 2)), dma((2,))] + gathers + reduces,
            compiler_params=params(2), name='last_block',
        )(x1, dy_loc, norm_gain, u1, gy_full, dah1, table, w_qkv, w_gate, w_up)

        grad_shapes = (rows_shape, shape((2 * width // 128, 128), F32)) + grad_shapes[2:]
        grad_x, gains, gqkv0, gout0, ggate0, gup0, gdown0 = pl.pallas_call(
            functools.partial(kernel_first_block, tp_size),
            out_shape=grad_shapes,
            in_specs=[vmem] * 4 + [anyspace] * 12,
            out_specs=(vmem, vmem) + (anyspace,) * 5,
            scratch_shapes=[
                pltpu.VMEM((seq, width), BF16), pltpu.VMEM((seq, width), BF16), pltpu.VMEM((width, cols), BF16), pltpu.VMEM((seq, cols), BF16),
                pltpu.VMEM((seq, HEAD_DIM + ff), BF16),
                pltpu.VMEM((seq, HEAD_DIM), BF16), pltpu.VMEM((seq, HEAD_DIM), BF16), pltpu.VMEM((seq, HEAD_DIM), BF16),
                pltpu.VMEM((seq, HEAD_DIM), F32), pltpu.VMEM((seq, HEAD_DIM), F32), pltpu.VMEM((seq, HEAD_DIM), F32),
                pltpu.VMEM((shard, width), F32), pltpu.VMEM((2, width // chips, cols), BF16),
                pltpu.VMEM((NP, HEAD_DIM + ff, piece_cols), BF16),
                pltpu.VMEM((2, 2 * width // 128, 128), F32), pltpu.VMEM((chips, 2 * width // 128, 128), F32),
                dma((32,)), dma((2, 3)), dma((NP, 2)), dma(()), dma(()), dma((chips - 1,)), dma((chips - 1,))] + gathers + gathers + reduces,
            compiler_params=params(3), name='first_block',
        )(x_loc, dx1, norm_gain, gain1, u0, q0, k0, v0, o0, ab0, table, w_qkv, w_out, w_gate, w_up, w_down)

        grad_gain = gains.reshape(2, width)
        return (grad_x, grad_gain, jnp.stack([gqkv0, gqkv1]), jnp.stack([gout0, gout1]), jnp.stack([ggate0, ggate1]),
                jnp.stack([gup0, gup1]), jnp.stack([gdown0, gdown1]))

    return jax.shard_map(device_program, mesh=mesh, in_specs=(row_spec, row_spec, P(None, None), col_spec, inner_spec, col_spec, col_spec, inner_spec), out_specs=(row_spec, P('dp', None), P('dp', None, 'tp'), P('dp', 'tp', None), P('dp', None, 'tp'), P('dp', None, 'tp'), P('dp', 'tp', None)), check_vma=False)
```

time: 854 us -> 534 us (0.63)
  Pallas kernels: 0 us -> 507 us
  waiting for transfers between devices: 435 us -> 0 us
  matrix products: 287 us -> 0 us
  blocking collectives: 43.8 us -> 0 us
  other arithmetic: 56.1 us -> 17.2 us
  between operations: 15.2 us -> 0.89 us
    pallas_call x0 -> x3, Pallas kernels: none -> 507 us  [the longest x1 178 us: device_program(): pl.pallas_call(functools.partial(kernel_first_block, tp_size), out_shape=...]
    dot_general x42 -> x0, matrix products: 287 us -> none  [the longest x2 39.6 us: block_backward(): jnp.einsum('sc,dc->sd', d_qkv, w_qkv_l, preferred_element_type=jnp.float32)]
    reduce_scatter x3 -> x0, waiting for transfers between devices: 225 us -> none  [the longest x2 130 us: block_backward(): lax.psum_scatter(normed_part, 'tp', scatter_dimension=0, tiled=True)]
    all_gather x6 -> x0, waiting for transfers between devices: 208 us -> none  [the longest x2 107 us: block_forward(): u_full = lax.all_gather(u_loc, 'tp', axis=0, tiled=True)]
    psum x1 -> x0, blocking collectives: 43.8 us -> none  [device_program(): grad_gain = lax.psum(jnp.stack([item[0] for item in layer_grads]), 'tp')]
    reduce_sum x8 -> x0, other arithmetic: 16.4 us -> none  [the longest x2 9.51 us: block_forward(): jnp.sum(jnp.exp(scores - row_max), axis=-1, keepdims=True)]
    another operation x11 -> x4, other arithmetic: 24.5 us -> 12 us  [the longest x1 3.69 us: device_program(): jnp.stack([ggate0, ggate1])]
    convert_element_type x8 -> x0, other arithmetic: 9.75 us -> none  [the longest x2 4.95 us: block_backward(): grad_x_loc = (dy_loc.astype(jnp.float32) + d_x_norm).astype(jnp.bfloat16)]
  transfers between devices with their start and end apart: 9 -> 0, of which waited for: 7 -> 0; matrix products, arithmetic and copies ran while one was open for 20% -> 0% of each run, Pallas kernels for 0% -> 0%
where the time goes in v1:
time: 534 us; the launch traced here: 530 us
  Pallas kernels  507 us (95%)
  other arithmetic  17.2 us (3%)
    pallas_call x1, Pallas kernels, device_program(): pl.pallas_call(functools.partial(kernel_first_block, tp_size), out_shape=...  178 us
    pallas_call x1, Pallas kernels, device_program(): pl.pallas_call(functools.partial(kernel_first, tp_size), out_shape=(rows_...  173 us
    pallas_call x1, Pallas kernels, device_program(): pl.pallas_call(functools.partial(kernel_last_block, tp_size), out_shape=g...  156 us

profile of v1, /device:TPU:21, one launch (start us, length us, event | category | flops | bytes accessed | tf_op | source)
XLA Modules:
  0.0 529.7 jit_solution(15045892551026555325)
XLA Ops:
  0.6 3.9 fusion.1
  4.5 1.3 pad_maximum_fusion.4.table_hbm
  5.8 173.1 %first_forward.1 = (bf16[128,2048]{1,0:T(8,128)(2,1)}, bf16[128,2048]{1,0:T(8,128)(2,1)}, bf16[128,2048]{1,0:T(8,128)(2,1)}, bf16[2048,2048]{1,0:T(8,128)(2,1)},...) custom-call(bf16[128,2048]{1,0:T(8,128)(2,1)} %x_ref.3, ...), custom_call_target="tpu_custom_call" | custom-call | tf_op jit(solution)/shard_map/first_forward/pallas_call | solution.py:877
  178.9 155.7 %last_block.1 = (bf16[128,2048]{1,0:T(8,128)(2,1)}, f32[1,2048]{1,0:T(1,128)}, bf16[2048,384]{1,0:T(8,128)(2,1)}, bf16[128,2048]{1,0:T(8,128)(2,1)}, bf16[2048,5...) custom-call(bf16[128,2048]{1,0:T(8,128)(2,1)} %get-tuple-element.31.x_ref, ...), custom_call_target="tpu_custom_call" | custom-call | tf_op jit(solution)/shard_map/last_block/pallas_call | solution.py:894
  334.6 178.0 %first_block.1 = (bf16[128,2048]{1,0:T(8,128)(2,1)}, f32[32,128]{1,0:T(8,128)}, bf16[2048,384]{1,0:T(8,128)(2,1)}, bf16[128,2048]{1,0:T(8,128)(2,1)}, bf16[2048,...) custom-call(bf16[128,2048]{1,0:T(8,128)(2,1)} %x_ref.3, ...), custom_call_target="tpu_custom_call" | custom-call | tf_op jit(solution)/shard_map/first_block/pallas_call | solution.py:911
  512.7 0.0 copy-start.6
  512.7 1.5 reshape.22
  514.1 2.3 pad_maximum_fusion.5
  516.4 0.0 copy-done.6
  516.4 0.0 copy-start.1
  516.4 3.6 pad_maximum_fusion.3
  520.0 0.0 copy-done
  520.0 0.0 copy-done.1
  520.0 0.0 copy-start.2
  520.0 0.0 copy-start.4
  520.0 0.0 copy-start.5
  520.0 2.5 pad_maximum_fusion.2
  522.5 0.0 copy-done.2
  522.5 1.2 copy-done.3
  523.7 0.6 copy-done.4
  524.4 0.6 copy-done.5
  525.0 3.7 pad_maximum_fusion
  528.7 0.0 copy-done.7
  528.7 0.8 copy.16
  (4 shorter events, 0.0 us)
Async XLA Ops:
  512.7 3.7 copy-start.6
  516.4 3.6 copy-start
  516.4 3.6 copy-start.1
  520.0 2.5 copy-start.2
  520.0 3.7 copy-start.3
  520.0 4.4 copy-start.4
  520.0 5.0 copy-start.5
  525.0 3.7 copy-start.7

commit v2 on v1

--- a/solution.py
+++ b/solution.py
@@ -2,6 +2,7 @@
 
 import jax
 import jax.numpy as jnp
+import numpy as np
 from jax import lax
 from jax.experimental import pallas as pl
 from jax.experimental.pallas import tpu as pltpu
@@ -129,7 +130,7 @@
         self.mate_wait(self.events + first, NP // 2)
 
     def mate_wait_chip(self, distance, rightward):
-        ring_first = lax.select(rightward, self.events, 0) + (distance - 1) * NP
+        ring_first = lax.select(rightward, self.events, 0) + jnp.maximum(distance - 1, 0) * NP
         self.mate_wait(lax.select(distance == 0, 2 * self.events, ring_first), NP)
 
     def finish(self):
@@ -148,91 +149,76 @@
 
 
 class Reduce:
+    SLOTS = 6
+
     def __init__(self, place, part, shard_rows, refs):
         self.place, self.part, self.shard = place, part, shard_rows
         self.events = (place.half - 1) * NP + NP // 2
-        self.ring_r, self.ring_l, self.acc, self.stage = refs[:4]
-        self.send_r, self.recv_r, self.send_l, self.recv_l, self.send_m, self.recv_m = refs[4:]
+        self.ring, self.acc, self.stage, self.send_n, self.recv_n, self.send_m, self.recv_m = refs
 
     @staticmethod
     def scratch(half, shard_rows, width):
         events = (half - 1) * NP + NP // 2
-        shapes = [(events,), (events,), (2 * events + NP,), (6, 2)]
-        sems = (events, events, events, events, 2 * events + NP, 2 * events + NP)
-        return [pltpu.VMEM(s + (shard_rows, width), F32) for s in shapes] + [pltpu.SemaphoreType.DMA((n,)) for n in sems]
-
-    def slot(self, event, way):
-        return lax.rem(event, 2) * 2 + way
-
-    def mate_copy(self, slot, index):
+        shapes = [(2, events), (2 * events + NP,), (Reduce.SLOTS, 2)]
+        sems = [(2, events), (2, events), (2 * events + NP,), (2 * events + NP,)]
+        return [pltpu.VMEM(s + (shard_rows, width), F32) for s in shapes] + [pltpu.SemaphoreType.DMA(s) for s in sems]
+
+    def mate_copy(self, term):
         return pltpu.make_async_remote_copy(
-            self.stage.at[slot, 1 - self.place.core], self.acc.at[index], self.send_m.at[index], self.recv_m.at[index],
+            self.stage.at[lax.rem(term, self.SLOTS), 1 - self.place.core], self.acc.at[term], self.send_m.at[term], self.recv_m.at[term],
             self.place.mate, MESH)
 
     def ring_copy(self, event, way):
-        if way == 0:
-            return pltpu.make_async_remote_copy(
-                self.acc.at[2 * event], self.ring_r.at[event], self.send_r.at[event], self.recv_r.at[event], self.place.right, MESH)
+        to = {'tp': self.place.near(1 - 2 * way) * 2 + self.place.core}
         return pltpu.make_async_remote_copy(
-            self.acc.at[2 * event + 1], self.ring_l.at[event], self.send_l.at[event], self.recv_l.at[event], self.place.left, MESH)
-
-    def fill(self, chip, piece, slot, index):
-        value = self.part(chip, piece)
+            self.acc.at[2 * event + way], self.ring.at[way, event], self.send_n.at[way, event], self.recv_n.at[way, event], to, MESH)
+
+    def fill(self, term):
+        @pl.when(term >= self.SLOTS)
+        def _():
+            self.mate_copy(jnp.maximum(term - self.SLOTS, 0)).wait_send()
+        slot = lax.rem(term, self.SLOTS)
+        way = lax.rem(term, 2)
+        shifted = lax.div(term, 2) + NP // 2
+        travels = term < 2 * self.events
+        distance = jnp.maximum(self.place.half - lax.div(shifted, NP), 0)
+        turn = lax.rem(shifted, NP)
+        piece = lax.select(travels, lax.select(way == 0, turn, NP - 1 - turn), lax.rem(jnp.maximum(term - 2 * self.events, 0), NP))
+        value = self.part(self.place.near((1 - 2 * way) * distance), piece)
         self.stage[slot, 0] = value[:self.shard]
         self.stage[slot, 1] = value[self.shard:]
-        self.mate_copy(slot, index).start()
-
-    def prepare(self, event, reuse=True):
-        shifted = event + NP // 2
-        distance = self.place.half - lax.div(shifted, NP)
-        piece = lax.rem(shifted, NP)
-        for way in range(2):
-            slot = self.slot(event, way)
-            if reuse:
-                self.mate_copy(slot, 2 * (event - 2) + way).wait_send()
-            if way == 0:
-                self.fill(self.place.near(distance), piece, slot, 2 * event)
-            else:
-                self.fill(self.place.near(-distance), NP - 1 - piece, slot, 2 * event + 1)
-
-    def prepare_own(self, second):
-        event = self.events + (1 if second else 0)
-        for way in range(2):
-            slot = 4 + way if second else self.slot(self.events, way)
-            if not second:
-                self.mate_copy(slot, 2 * (event - 2) + way).wait_send()
-            self.fill(self.place.chip, (2 if second else 0) + way, slot, 2 * event + way)
-
-    def event(self, event, arrives):
-        for way in range(2):
-            index = 2 * event + way
-            slot = self.slot(event, way)
-            self.mate_copy(slot, index).wait_recv()
-            total = self.stage[slot, self.place.core] + self.acc[index]
-            if arrives:
-                self.ring_copy(event - NP, way).wait_recv()
-                ring = self.ring_r if way == 0 else self.ring_l
-                total = total + ring[event - NP]
-            self.acc[index] = total
+        self.mate_copy(term).start()
+
+    def event(self, event):
+        def add(way, carry):
+            term = 2 * event + way
+            self.mate_copy(term).wait_recv()
+            self.acc[term] += self.stage[lax.rem(term, self.SLOTS), self.place.core]
+
+            @pl.when(event >= NP)
+            def _():
+                before = jnp.maximum(event - NP, 0)
+                self.ring_copy(before, way).wait_recv()
+                self.acc[term] += self.ring[way, before]
             self.ring_copy(event, way).start()
+            return carry
+        lax.fori_loop(0, 2, add, 0)
 
     def final(self, piece):
         last = self.events - NP
-        index = 2 * self.events + piece
-        slot = piece % 2 + (4 if piece >= 2 else 2 * (self.events % 2))
-        self.mate_copy(slot, index).wait_recv()
+        term = 2 * self.events + piece
+        self.mate_copy(term).wait_recv()
         self.ring_copy(last + piece, 0).wait_recv()
         self.ring_copy(last + NP - 1 - piece, 1).wait_recv()
-        return ((self.stage[slot, self.place.core] + self.acc[index])
-                + (self.ring_r[last + piece] + self.ring_l[last + NP - 1 - piece]))
-
-    def final_order(self):
-        return range(NP)
+        return ((self.stage[term % self.SLOTS, self.place.core] + self.acc[term])
+                + (self.ring[0, last + piece] + self.ring[1, last + NP - 1 - piece]))
 
     def finish(self):
-        for event in range(self.events - 1, self.events + 2):
-            for way in range(2):
-                self.mate_copy(0, 2 * event + way).wait_send()
+        def across(term, carry):
+            self.mate_copy(term).wait_send()
+            return carry
+        terms = 2 * self.events + NP
+        lax.fori_loop(terms - self.SLOTS, terms, across, 0)
 
         def ring(event, carry):
             self.ring_copy(event, 0).wait_send()
@@ -241,39 +227,24 @@
         lax.fori_loop(0, self.events, ring, 0)
 
     def run(self, filler):
-        self.prepare(0, reuse=False)
-
-        def first(event, carry):
-            self.event(event, False)
-
-            @pl.when(event < 1)
+        def body(turn, carry):
+            event = jnp.maximum(turn - 1, 0)
+            travels = (turn >= 1) & (turn <= self.events)
+
+            @pl.when(travels)
             def _():
-                self.prepare(event + 1, reuse=False)
-
-            @pl.when(event >= 1)
+                self.event(event)
+
+            def ahead(way, inner):
+                self.fill(2 * turn + way)
+                return inner
+            lax.fori_loop(0, 2, ahead, 0)
+
+            @pl.when(travels)
             def _():
-                self.prepare(event + 1)
-            filler(event)
+                filler(event)
             return carry
-
-        def later(event, carry):
-            self.event(event, True)
-
-            @pl.when(event + 1 < self.events)
-            def _():
-                self.prepare(event + 1)
-
-            @pl.when(event + 1 == self.events)
-            def _():
-                self.prepare_own(False)
-
-            @pl.when(event == NP)
-            def _():
-                self.prepare_own(True)
-            filler(event)
-            return carry
-        lax.fori_loop(0, NP, first, 0)
-        lax.fori_loop(NP, self.events, later, 0)
+        lax.fori_loop(0, self.events + 2, body, 0)
 
 
 def rope_pair(table):
@@ -281,6 +252,23 @@
     swapped = pltpu.roll(table, HEAD_DIM // 2, 1)
     low = lanes < HEAD_DIM // 2
     return jnp.where(low, table, swapped), jnp.where(low, -swapped, table)
+
+
+def fill_table(freqs, table_ref):
+    rows = 64
+    blocks = table_ref.shape[0] // rows
+
+    def cos_sin(count, scale):
+        steps = lax.broadcasted_iota(jnp.int32, (count, HEAD_DIM), 0) * scale
+        angles = steps.astype(F32) * freqs
+        return jnp.cos(angles), jnp.sin(angles)
+    cos_low, sin_low = cos_sin(rows, 1)
+    cos_high, sin_high = cos_sin(max(blocks, 8), rows)
+    low = lax.broadcasted_iota(jnp.int32, (1, HEAD_DIM), 1) < HEAD_DIM // 2
+    first = jnp.where(low, cos_high, sin_high)
+    second = jnp.where(low, -sin_high, cos_high)
+    for block in range(blocks):
+        table_ref[block * rows:(block + 1) * rows] = first[block:block + 1] * cos_low + second[block:block + 1] * sin_low
 
 
 def rope(values, table, inverse=False):
@@ -357,26 +345,42 @@
         return copy
 
 
-def gather_units(gather, unit, event):
-    step = lax.div(event, NP) + 1
-    piece = lax.rem(event, NP)
-    last = gather.events - 1
-    own = event == 1
-    near = (event >= NP) & (lax.rem(event, 2) == 0)
-    final = event == last
-
-    @pl.when(own | near | final)
-    def _():
-        distance = step - 1
-        rightward = final | (piece != 0)
-        gather.mate_wait_chip(distance, rightward)
-        chip = gather.place.near(lax.select(rightward, distance, -distance))
-        unit(chip)
-
-
-def kernel_first(tp_size, x_ref, gain_ref, gy_hbm, table_hbm, wqkv_hbm, wout_hbm, wgate_hbm, wup_hbm, wdown_hbm,
-                 x1_out, u1_out, u0_out, gy_out, q_out, k_out, v_out, o_out, ab_out, dah_out, *scratch):
-    n_gather, n_reduce = 6, 10
+def gather_loop(gather, unit, then=None):
+    chips = gather.place.ring
+
+    def body(event, carry):
+        @pl.when(event < gather.events)
+        def _():
+            gather.event(event)
+            if then is not None:
+                then(event)
+        step = lax.div(event, NP) + 1
+        opposite = event == gather.events
+        final = event == gather.events - 1
+        own = event == 1
+        near = (event >= NP) & (event < gather.events) & (lax.rem(event, 2) == 0)
+
+        @pl.when(opposite)
+        def _():
+            gather.mate_wait_last()
+
+        @pl.when(own | near | final)
+        def _():
+            gather.mate_wait_chip(step - 1, final | (lax.rem(event, NP) != 0))
+
+        @pl.when(own | near | final | opposite)
+        def _():
+            distance = lax.select(opposite, gather.place.half, step - 1)
+            rightward = final | (lax.rem(event, NP) != 0)
+            count = lax.select(own, 0, lax.select(opposite, chips - 1, lax.select(final, chips - 2, jnp.maximum(lax.div(event, 2) - 1, 0))))
+            unit(count, gather.place.near(lax.select(rightward, distance, -distance)))
+        return carry
+    lax.fori_loop(0, gather.events + 1, body, 0)
+
+
+def kernel_first(tp_size, x_ref, gain_ref, freq_ref, gy_hbm, wqkv_hbm, wout_hbm, wgate_hbm, wup_hbm, wdown_hbm,
+                 x1_out, u1_out, u0_out, gy_out, q_out, k_out, v_out, o_out, ab_out, dah_out, table_out, *scratch):
+    n_gather = 6
     (u_ref, g_ref, wc_ref, wo_ref, wo1_ref, q_ref, k_ref, v_ref, om_ref, ab_ref, dah_ref, table_ref, y_ref, local) = scratch[:14]
     sems_u = scratch[14:14 + n_gather]
     sems_g = scratch[14 + n_gather:14 + 2 * n_gather]
@@ -395,8 +399,7 @@
     load_g = loads.start(gy_hbm, g_ref.at[gg.own_rows()])
     load_w = [loads.start(wqkv_hbm.at[0], wc_ref.at[:, 0:head_cols]),
               loads.start(wgate_hbm.at[0], wc_ref.at[:, head_cols:head_cols + ff]),
-              loads.start(wup_hbm.at[0], wc_ref.at[:, head_cols + ff:head_cols + 2 * ff]),
-              loads.start(table_hbm, table_ref)]
+              loads.start(wup_hbm.at[0], wc_ref.at[:, head_cols + ff:head_cols + 2 * ff])]
     load_o = []
     for piece in range(NP):
         cols = slice(piece * piece_cols, (piece + 1) * piece_cols)
@@ -411,6 +414,7 @@
     u0_out[...] = u_own
     place.barrier()
     gu.start()
+    fill_table(freq_ref[0:1], table_ref)
     load_g.wait()
     for copy in load_w:
         copy.wait()
@@ -441,20 +445,11 @@
         om_ref[here, HEAD_DIM:HEAD_DIM + ff] = (gate_f * jax.nn.sigmoid(gate_f) * up_f).astype(BF16)
         ab_copy(slot, here).start()
 
-    def unit_count(event):
-        return lax.select(event == 1, 0, lax.select(event == gu.events - 1, chips - 2, lax.div(event, 2) - 1))
-
-    def loop_u(event, carry):
-        gu.event(event)
-
+    def start_gy(event):
         @pl.when(event == gu.events - NP)
         def _():
             gg.start()
-        gather_units(gu, functools.partial(unit, unit_count(event)), event)
-        return carry
-    lax.fori_loop(0, gu.events, loop_u, 0)
-    gu.mate_wait_last()
-    unit(jnp.int32(chips - 1), place.near(place.half))
+    gather_loop(gu, unit, start_gy)
 
     def write_o(here, value):
         om_ref[here, 0:HEAD_DIM] = value
@@ -476,7 +471,7 @@
     outs = Copies(local)
     outs.used = n_out + 2
     saves = [outs.start(q_ref, q_out), outs.start(k_ref, k_out), outs.start(v_ref, v_out),
-             outs.start(om_ref.at[:, 0:HEAD_DIM], o_out)]
+             outs.start(om_ref.at[:, 0:HEAD_DIM], o_out), outs.start(table_ref, table_out)]
     n_dah = outs.used + 1
 
     def gy_copy():
@@ -503,7 +498,7 @@
 
         @pl.when((event >= NP) & (event < NP + chips))
         def _():
-            block = event - NP
+            block = jnp.maximum(event - NP, 0)
             here = pl.ds(aligned(block * pair, pair), pair)
             slot = lax.rem(block, 2)
 
@@ -514,7 +509,7 @@
             dah_copy(slot, here).start()
 
     reduce.run(filler)
-    for piece in reduce.final_order():
+    for piece in range(NP):
         y_ref[:, piece * piece_cols:(piece + 1) * piece_cols] = reduce.final(piece)
     x_next = (x_ref[...].astype(F32) + y_ref[...]).astype(BF16)
     x1_out[...] = x_next
@@ -609,7 +604,7 @@
     for copy in load_w:
         copy.wait()
 
-    def unit(chip):
+    def unit(count, chip):
         here = pl.ds(aligned(chip * pair, pair), pair)
         rows_u = u_ref[here]
         qkv = dot_nn(rows_u, wc_ref[:, 0:head_cols]).astype(BF16)
@@ -625,13 +620,7 @@
         dx_ref[here, head_cols:head_cols + ff] = d_gate
         dx_ref[here, head_cols + ff:head_cols + 2 * ff] = d_up
 
-    def loop_u(event, carry):
-        gu.event(event)
-        gather_units(gu, unit, event)
-        return carry
-    lax.fori_loop(0, gu.events, loop_u, 0)
-    gu.mate_wait_last()
-    unit(place.near(place.half))
+    gather_loop(gu, unit)
 
     def read_da(here):
         return ho_ref[here, 0:HEAD_DIM]
@@ -671,10 +660,10 @@
 
         @pl.when((event >= NP) & (event < NP + chips))
         def _():
-            weight_grads_u(event - NP, u_ref, dx_ref, gs_ref, outs_u, sems_gs, head_cols, ff)
+            weight_grads_u(jnp.maximum(event - NP, 0), u_ref, dx_ref, gs_ref, outs_u, sems_gs, head_cols, ff)
 
     reduce.run(filler)
-    for piece in reduce.final_order():
+    for piece in range(NP):
         y_ref[:, piece * piece_cols:(piece + 1) * piece_cols] = reduce.final(piece)
     d_normed = y_ref[...].astype(BF16).astype(F32)
     d_x, gain_part = norm_backward(x_ref[...].astype(F32), gain_ref[1:2], d_normed)
@@ -732,7 +721,7 @@
     for copy in load_h:
         copy.wait()
 
-    def unit(chip):
+    def unit(count, chip):
         here = pl.ds(aligned(chip * pair, pair), pair)
         dah = dot_nt(g_ref[here, 0:piece_cols], hs_ref[0])
         for piece in range(1, NP):
@@ -746,17 +735,11 @@
         dx_ref[here, head_cols:head_cols + ff] = d_gate
         dx_ref[here, head_cols + ff:head_cols + 2 * ff] = d_up
 
-    def loop_g(event, carry):
-        gg.event(event)
-
+    def start_u(event):
         @pl.when(event == gg.events - NP)
         def _():
             gu.start()
-        gather_units(gg, unit, event)
-        return carry
-    lax.fori_loop(0, gg.events, loop_g, 0)
-    gg.mate_wait_last()
-    unit(place.near(place.half))
+    gather_loop(gg, unit, start_u)
     for copy in load_a:
         copy.wait()
 
@@ -802,10 +785,10 @@
 
         @pl.when((event >= NP) & (event < NP + chips))
         def _():
-            weight_grads_u(event - NP, u_ref, dx_ref, gs_ref, outs_u, sems_gs, head_cols, ff)
+            weight_grads_u(jnp.maximum(event - NP, 0), u_ref, dx_ref, gs_ref, outs_u, sems_gs, head_cols, ff)
 
     reduce.run(filler)
-    for piece in reduce.final_order():
+    for piece in range(NP):
         y_ref[:, piece * piece_cols:(piece + 1) * piece_cols] = reduce.final(piece)
     d_normed = y_ref[...].astype(BF16).astype(F32)
     d_x, gain_part = norm_backward(x_ref[...].astype(F32), gain_ref[0:1], d_normed)
@@ -839,7 +822,26 @@
     total = all_ref[0]
     for chip in range(1, chips):
         total = total + all_ref[chip]
-    gain_out[...] = total
+    for tile in range(tiles):
+        for layer in range(2):
+            gain_out[layer:layer + 1, tile * lanes:(tile + 1) * lanes] = total[layer * tiles + tile:layer * tiles + tile + 1]
+
+
+def kernel_stack(*refs):
+    lasts, firsts, outs, bufs, (sem_in, sem_out) = refs[0:5], refs[5:10], refs[10:15], refs[15:20], refs[20:22]
+    reads, writes = [], []
+    for layer, sources in ((1, lasts), (0, firsts)):
+        for number, source in enumerate(sources):
+            slot = len(reads)
+            reads.append(pltpu.make_async_copy(source, bufs[number].at[layer], sem_in.at[slot]))
+            writes.append(pltpu.make_async_copy(bufs[number].at[layer], outs[number].at[layer], sem_out.at[slot]))
+    for read in reads:
+        read.start()
+    for read, write in zip(reads, writes):
+        read.wait()
+        write.start()
+    for write in writes:
+        write.wait()
 
 
 def solution(mesh):
@@ -862,10 +864,8 @@
         shape = jax.ShapeDtypeStruct
         dma = pltpu.SemaphoreType.DMA
 
-        half_dim = HEAD_DIM // 2
-        freqs = ROPE_BASE ** (-2.0 * jnp.arange(half_dim, dtype=F32) / HEAD_DIM)
-        angles = jnp.arange(seq, dtype=F32)[:, None] * freqs[None, :]
-        table = jnp.concatenate([jnp.cos(angles), jnp.sin(angles)], axis=1)
+        freqs = np.float32(ROPE_BASE) ** (np.float32(-2.0) * np.arange(HEAD_DIM // 2, dtype=np.float32) / np.float32(HEAD_DIM))
+        freqs = jnp.asarray(np.tile(freqs, (8, 2)))
 
         def params(number):
             return pltpu.CompilerParams(collective_id=number, has_side_effects=True, vmem_limit_bytes=67043328)
@@ -874,12 +874,12 @@
         head_shape = shape((seq, HEAD_DIM), BF16)
         gathers = Gather.scratch(half)
         reduces = Reduce.scratch(half, shard, piece_cols)
-        x1, u1, u0, gy_full, q0, k0, v0, o0, ab0, dah1 = pl.pallas_call(
+        x1, u1, u0, gy_full, q0, k0, v0, o0, ab0, dah1, table = pl.pallas_call(
             functools.partial(kernel_first, tp_size),
             out_shape=(rows_shape, rows_shape, rows_shape, shape((seq, width), BF16), head_shape, head_shape, head_shape, head_shape,
-                       shape((seq, 2 * ff), BF16), shape((seq, HEAD_DIM + ff), BF16)),
-            in_specs=[vmem, vmem] + [anyspace] * 7,
-            out_specs=(vmem, vmem, vmem) + (anyspace,) * 7,
+                       shape((seq, 2 * ff), BF16), shape((seq, HEAD_DIM + ff), BF16), shape((seq, HEAD_DIM), F32)),
+            in_specs=[vmem, vmem, vmem] + [anyspace] * 6,
+            out_specs=(vmem, vmem, vmem) + (anyspace,) * 8,
             scratch_shapes=[
                 pltpu.VMEM((seq, width), BF16), pltpu.VMEM((seq, width), BF16), pltpu.VMEM((width, cols), BF16),
                 pltpu.VMEM((NP, HEAD_DIM + ff, piece_cols), BF16), pltpu.VMEM((HEAD_DIM + ff, width), BF16),
@@ -887,7 +887,7 @@
                 pltpu.VMEM((seq, HEAD_DIM + ff), BF16), pltpu.VMEM((2, pair, 2 * ff), BF16), pltpu.VMEM((2, pair, HEAD_DIM + ff), BF16),
                 pltpu.VMEM((seq, HEAD_DIM), F32), pltpu.VMEM((shard, width), F32), dma((32,))] + gathers + gathers + reduces,
             compiler_params=params(1), name='first_forward',
-        )(x_loc, norm_gain, dy_loc, table, w_qkv, w_out, w_gate, w_up, w_down)
+        )(x_loc, norm_gain, freqs, dy_loc, w_qkv, w_out, w_gate, w_up, w_down)
 
         grad_shapes = (rows_shape, shape((1, width), F32), shape((width, head_cols), BF16), shape((HEAD_DIM, width), BF16),
                        shape((width, ff), BF16), shape((width, ff), BF16), shape((ff, width), BF16))
@@ -907,8 +907,8 @@
             compiler_params=params(2), name='last_block',
         )(x1, dy_loc, norm_gain, u1, gy_full, dah1, table, w_qkv, w_gate, w_up)
 
-        grad_shapes = (rows_shape, shape((2 * width // 128, 128), F32)) + grad_shapes[2:]
-        grad_x, gains, gqkv0, gout0, ggate0, gup0, gdown0 = pl.pallas_call(
+        grad_shapes = (rows_shape, shape((2, width), F32)) + grad_shapes[2:]
+        grad_x, grad_gain, gqkv0, gout0, ggate0, gup0, gdown0 = pl.pallas_call(
             functools.partial(kernel_first_block, tp_size),
             out_shape=grad_shapes,
             in_specs=[vmem] * 4 + [anyspace] * 12,
@@ -925,8 +925,15 @@
             compiler_params=params(3), name='first_block',
         )(x_loc, dx1, norm_gain, gain1, u0, q0, k0, v0, o0, ab0, table, w_qkv, w_out, w_gate, w_up, w_down)
 
-        grad_gain = gains.reshape(2, width)
-        return (grad_x, grad_gain, jnp.stack([gqkv0, gqkv1]), jnp.stack([gout0, gout1]), jnp.stack([ggate0, ggate1]),
-                jnp.stack([gup0, gup1]), jnp.stack([gdown0, gdown1]))
+        firsts, lasts = (gqkv0, gout0, ggate0, gup0, gdown0), (gqkv1, gout1, ggate1, gup1, gdown1)
+        stacked = pl.pallas_call(
+            kernel_stack,
+            out_shape=tuple(shape((2,) + first.shape, BF16) for first in firsts),
+            in_specs=[anyspace] * 10,
+            out_specs=(anyspace,) * 5,
+            scratch_shapes=[pltpu.VMEM((2,) + first.shape, BF16) for first in firsts] + [dma((10,)), dma((10,))],
+            compiler_params=pltpu.CompilerParams(vmem_limit_bytes=40 * 2 ** 20), name='stack',
+        )(*lasts, *firsts)
+        return (grad_x, grad_gain) + tuple(stacked)
 
     return jax.shard_map(device_program, mesh=mesh, in_specs=(row_spec, row_spec, P(None, None), col_spec, inner_spec, col_spec, col_spec, inner_spec), out_specs=(row_spec, P('dp', None), P('dp', None, 'tp'), P('dp', 'tp', None), P('dp', None, 'tp'), P('dp', None, 'tp'), P('dp', 'tp', None)), check_vma=False)

time: 534 us -> 529 us (level)
  other arithmetic: 17.2 us -> 0 us
  Pallas kernels: 507 us -> 515 us
  local copies, waits for them, and re-layouts: 4.73 us -> 12.7 us
    another operation x4 -> x0, other arithmetic: 12 us -> none  [the longest x1 3.69 us: device_program(): jnp.stack([ggate0, ggate1])]
    unnamed x17 -> x22, local copies, waits for them, and re-layouts: 3.27 us -> 12.7 us
    pallas_call x0 -> x1, Pallas kernels: none -> 7.72 us  [device_program(): pl.pallas_call(kernel_stack, out_shape=tuple((shape((2,) + first.shape, B...]
where the time goes in v2:
time: 529 us; the launch traced here: 528 us
  Pallas kernels  515 us (97%)
  local copies, waits for them, and re-layouts  12.7 us (2%)
    pallas_call x1, Pallas kernels, device_program(): pl.pallas_call(functools.partial(kernel_first_block, tp_size), out_shape=...  178 us
    pallas_call x1, Pallas kernels, device_program(): pl.pallas_call(functools.partial(kernel_first, tp_size), out_shape=(rows_...  173 us
    pallas_call x1, Pallas kernels, device_program(): pl.pallas_call(functools.partial(kernel_last_block, tp_size), out_shape=g...  156 us
    unnamed x22, local copies, waits for them, and re-layouts  12.7 us

profile of v2, /device:TPU:21, one launch (start us, length us, event | category | flops | bytes accessed | tf_op | source)
XLA Modules:
  0.0 528.3 jit_solution(9819118301202445033)
XLA Ops:
  0.6 173.2 %first_forward.1 = (bf16[128,2048]{1,0:T(8,128)(2,1)}, bf16[128,2048]{1,0:T(8,128)(2,1)}, bf16[128,2048]{1,0:T(8,128)(2,1)}, bf16[2048,2048]{1,0:T(8,128)(2,1)},...) custom-call(bf16[128,2048]{1,0:T(8,128)(2,1)} %x_ref.3, ...), custom_call_target="tpu_custom_call" | custom-call | tf_op jit(solution)/shard_map/first_forward/pallas_call | solution.py:877
  173.8 155.9 %last_block.1 = (bf16[128,2048]{1,0:T(8,128)(2,1)}, f32[1,2048]{1,0:T(1,128)}, bf16[2048,384]{1,0:T(8,128)(2,1)}, bf16[128,2048]{1,0:T(8,128)(2,1)}, bf16[2048,5...) custom-call(bf16[128,2048]{1,0:T(8,128)(2,1)} %get-tuple-element.37.x_ref, ...), custom_call_target="tpu_custom_call" | custom-call | tf_op jit(solution)/shard_map/last_block/pallas_call | solution.py:894
  329.8 178.1 %first_block.1 = (bf16[128,2048]{1,0:T(8,128)(2,1)}, f32[2,2048]{1,0:T(2,128)}, bf16[2048,384]{1,0:T(8,128)(2,1)}, bf16[128,2048]{1,0:T(8,128)(2,1)}, bf16[2048,...) custom-call(bf16[128,2048]{1,0:T(8,128)(2,1)} %x_ref.3, ...), custom_call_target="tpu_custom_call" | custom-call | tf_op jit(solution)/shard_map/first_block/pallas_call | solution.py:911
  507.9 0.0 copy-start
  507.9 1.6 copy-done
  509.5 0.0 copy-start.1
  509.5 1.6 copy-done.1
  511.1 0.0 copy-start.2
  511.1 1.6 copy-done.2
  512.7 0.0 copy-start.3
  512.7 1.6 copy-done.3
  514.3 0.0 copy-start.4
  514.3 1.4 copy-done.4
  515.7 0.0 copy-start.5
  515.7 1.4 copy-done.5
  517.1 0.0 copy-start.6
  517.1 1.0 copy-done.6
  518.1 0.0 copy-start.7
  518.1 1.0 copy-done.7
  519.2 7.7 %stack.1 = (bf16[2,2048,384]{2,1,0:T(8,128)(2,1)}, bf16[2,128,2048]{2,1,0:T(8,128)(2,1)}, bf16[2,2048,512]{2,1,0:T(8,128)(2,1)}, bf16[2,2048,512]{2,1,0:T(8,128)(2,1)}, bf16[2,512,2048]{2,1,0:T(8,128)(2,1)}) custom-call(bf16[2048,384]{1,0:T(8,128)(2,1)S(1)} %copy-done.4, bf16[128,2048]{1,0:T(8,128)(2,1)S(1)} %copy-done.6, bf16[2048,512]{1,0:T(8,128)(2,1)S(1)} %copy-done, ...), custom_call_target="tpu_custom_call" | custom-call | tf_op jit(solution)/shard_map/stack/pallas_call | solution.py:929
  526.9 0.0 copy-done.8
  526.9 0.8 copy.18
  527.7 0.0 copy-done.9
  527.7 0.6 copy.19
  (2 shorter events, 0.0 us)
Async XLA Ops:
  507.9 1.6 copy-start
  509.5 1.6 copy-start.1
  511.1 1.6 copy-start.2
  512.7 1.6 copy-start.3
  514.3 1.4 copy-start.4
  515.7 1.4 copy-start.5
  517.1 1.0 copy-start.6
  518.1 1.0 copy-start.7
  519.2 7.7 %copy-start.8 = (bf16[128,2048]{1,0:T(8,128)(2,1)S(1)}, bf16[128,2048]{1,0:T(8,128)(2,1)}, u32[]{:S(2)}) copy-start(bf16[128,2048]{1,0:T(8,128)(2,1)} %get-tuple-element.74) | copy-start | bytes 1572868
  519.2 8.5 %copy-start.9 = (f32[2,2048]{1,0:T(2,128)S(1)}, f32[2,2048]{1,0:T(2,128)}, u32[]{:S(2)}) copy-start(f32[2,2048]{1,0:T(2,128)} %get-tuple-element.75) | copy-start | bytes 49156

commit v3 on v2

v3 whole, which is shorter than its diff:
```python
import functools

import jax
import jax.numpy as jnp
import numpy as np
from jax import lax
from jax.experimental import pallas as pl
from jax.experimental.pallas import tpu as pltpu
from jax.sharding import PartitionSpec as P

HEAD_DIM = 128
NORM_EPS = 1e-5
ROPE_BASE = 10000.0
MESH = pl.DeviceIdType.MESH
NP = 4
F32 = jnp.float32
BF16 = jnp.bfloat16


def dot_nn(a, b):
    return lax.dot_general(a, b, (((1,), (0,)), ((), ())), preferred_element_type=F32)


def dot_nt(a, b):
    return lax.dot_general(a, b, (((1,), (1,)), ((), ())), preferred_element_type=F32)


def dot_tn(a, b):
    return lax.dot_general(a, b, (((0,), (0,)), ((), ())), preferred_element_type=F32)


def aligned(index, size):
    return pl.multiple_of(index, size)


class Place:
    def __init__(self, tp_size):
        index = lax.axis_index('tp')
        self.ring = tp_size // 2
        self.half = self.ring // 2
        self.core = lax.rem(index, 2)
        self.chip = lax.div(index, 2)
        self.right = {'tp': self.near(1) * 2 + self.core}
        self.left = {'tp': self.near(-1) * 2 + self.core}
        self.mate = {'tp': self.chip * 2 + 1 - self.core}

    def near(self, step):
        return lax.rem(self.chip + step + self.ring, self.ring)

    def barrier(self, others=()):
        sem = pltpu.get_barrier_semaphore()
        peers = [self.right, self.left, self.mate] + list(others)
        for peer in peers:
            pl.semaphore_signal(sem, inc=1, device_id=peer, device_id_type=MESH)
        pl.semaphore_wait(sem, len(peers))


class Gather:
    def __init__(self, place, buf, shard_rows, sems):
        self.place, self.buf, self.shard = place, buf, shard_rows
        self.rows = shard_rows // NP
        self.events = (place.half - 1) * NP + NP // 2
        self.send_r, self.recv_r, self.send_l, self.recv_l, self.send_m, self.recv_m = sems

    @staticmethod
    def scratch(half):
        events = (half - 1) * NP + NP // 2
        return [pltpu.SemaphoreType.DMA((n,)) for n in (events, events, events, events, 2 * events + NP, 2 * events + NP)]

    def view(self, chip, core, piece):
        start = (chip * 2 + core) * self.shard + piece * self.rows
        return self.buf.at[pl.ds(aligned(start, self.rows), self.rows)]

    def own_rows(self):
        start = (self.place.chip * 2 + self.place.core) * self.shard
        return pl.ds(aligned(start, self.shard), self.shard)

    def to_right(self, event, view):
        return pltpu.make_async_remote_copy(view, view, self.send_r.at[event], self.recv_r.at[event], self.place.right, MESH)

    def to_left(self, event, view):
        return pltpu.make_async_remote_copy(view, view, self.send_l.at[event], self.recv_l.at[event], self.place.left, MESH)

    def to_mate(self, slot, view):
        return pltpu.make_async_remote_copy(view, view, self.send_m.at[slot], self.recv_m.at[slot], self.place.mate, MESH)

    def start(self):
        place = self.place
        for piece in range(NP):
            self.to_right(piece, self.view(place.chip, place.core, piece)).start()
            self.to_left(piece, self.view(place.chip, place.core, NP - 1 - piece)).start()
        for piece in range(NP):
            self.to_mate(2 * self.events + piece, self.view(place.chip, place.core, piece)).start()

    def views(self, event):
        step = lax.div(event, NP) + 1
        piece = lax.rem(event, NP)
        from_left = self.view(self.place.near(-step), self.place.core, piece)
        from_right = self.view(self.place.near(step), self.place.core, NP - 1 - piece)
        return from_left, from_right

    def event(self, event, forward=None):
        from_left, from_right = self.views(event)
        self.to_right(event, from_left).wait_recv()
        self.pass_on(event, forward, lambda: self.to_right(event + NP, from_left).start())
        self.to_mate(event, from_left).start()
        self.to_left(event, from_right).wait_recv()
        self.pass_on(event, forward, lambda: self.to_left(event + NP, from_right).start())
        self.to_mate(self.events + event, from_right).start()

    def pass_on(self, event, forward, send):
        if forward is None:
            pl.when(event + NP < self.events)(send)
        elif forward:
            send()

    def mate_wait(self, first, count):
        for offset in range(count):
            self.to_mate(first + offset, self.view(self.place.chip, 1 - self.place.core, 0)).wait_recv()

    def mate_wait_all(self):
        def body(slot, carry):
            self.mate_wait(slot, 1)
            return carry
        lax.fori_loop(0, 2 * self.events + NP, body, 0)

    def mate_wait_last(self):
        first = (self.place.half - 1) * NP
        self.mate_wait(first, NP // 2)
        self.mate_wait(self.events + first, NP // 2)

    def mate_wait_chip(self, distance, rightward):
        ring_first = lax.select(rightward, self.events, 0) + jnp.maximum(distance - 1, 0) * NP
        self.mate_wait(lax.select(distance == 0, 2 * self.events, ring_first), NP)

    def finish(self):
        view = self.view(self.place.chip, self.place.core, 0)

        def ring(event, carry):
            self.to_right(event, view).wait_send()
            self.to_left(event, view).wait_send()
            return carry
        lax.fori_loop(0, self.events, ring, 0)

        def across(slot, carry):
            self.to_mate(slot, view).wait_send()
            return carry
        lax.fori_loop(0, 2 * self.events + NP, across, 0)


class Reduce:
    SLOTS = 6
    DEPTH = 8

    def __init__(self, place, part, shard_rows, refs):
        self.place, self.part, self.shard = place, part, shard_rows
        self.events = (place.half - 1) * NP + NP // 2
        self.ring, self.acc, self.stage, self.send_n, self.recv_n, self.send_m, self.recv_m = refs

    @staticmethod
    def scratch(half, shard_rows, width):
        events = (half - 1) * NP + NP // 2
        shapes = [(2, events), (2 * Reduce.DEPTH + NP,), (Reduce.SLOTS, 2)]
        sems = [(2, events), (2, events), (2 * events + NP,), (2 * events + NP,)]
        return [pltpu.VMEM(s + (shard_rows, width), F32) for s in shapes] + [pltpu.SemaphoreType.DMA(s) for s in sems]

    def acc_slot(self, term):
        own = 2 * self.DEPTH + jnp.maximum(term - 2 * self.events, 0)
        return lax.select(term < 2 * self.events, lax.rem(term, 2 * self.DEPTH), own)

    def mate_copy(self, term):
        return pltpu.make_async_remote_copy(
            self.stage.at[lax.rem(term, self.SLOTS), 1 - self.place.core], self.acc.at[self.acc_slot(term)], self.send_m.at[term], self.recv_m.at[term],
            self.place.mate, MESH)

    def ring_copy(self, event, way):
        to = {'tp': self.place.near(1 - 2 * way) * 2 + self.place.core}
        return pltpu.make_async_remote_copy(
            self.acc.at[self.acc_slot(2 * event + way)], self.ring.at[way, event], self.send_n.at[way, event], self.recv_n.at[way, event], to, MESH)

    def fill(self, term):
        @pl.when(term >= self.SLOTS)
        def _():
            self.mate_copy(jnp.maximum(term - self.SLOTS, 0)).wait_send()
        slot = lax.rem(term, self.SLOTS)
        way = lax.rem(term, 2)

        @pl.when(term >= 2 * (self.DEPTH - 1))
        def _():
            self.ring_copy(jnp.maximum(lax.div(term, 2) - (self.DEPTH - 1), 0), way).wait_send()
        shifted = lax.div(term, 2) + NP // 2
        travels = term < 2 * self.events
        distance = jnp.maximum(self.place.half - lax.div(shifted, NP), 0)
        turn = lax.rem(shifted, NP)
        piece = lax.select(travels, lax.select(way == 0, turn, NP - 1 - turn), lax.rem(jnp.maximum(term - 2 * self.events, 0), NP))
        value = self.part(self.place.near((1 - 2 * way) * distance), piece)
        self.stage[slot, 0] = value[:self.shard]
        self.stage[slot, 1] = value[self.shard:]
        self.mate_copy(term).start()

    def event(self, event):
        def add(way, carry):
            term = 2 * event + way
            self.mate_copy(term).wait_recv()
            slot = self.acc_slot(term)
            self.acc[slot] += self.stage[lax.rem(term, self.SLOTS), self.place.core]

            @pl.when(event >= NP)
            def _():
                before = jnp.maximum(event - NP, 0)
                self.ring_copy(before, way).wait_recv()
                self.acc[slot] += self.ring[way, before]
            self.ring_copy(event, way).start()
            return carry
        lax.fori_loop(0, 2, add, 0)

    def final(self, piece):
        last = self.events - NP
        term = 2 * self.events + piece
        self.mate_copy(term).wait_recv()
        self.ring_copy(last + piece, 0).wait_recv()
        self.ring_copy(last + NP - 1 - piece, 1).wait_recv()
        return ((self.stage[term % self.SLOTS, self.place.core] + self.acc[2 * self.DEPTH + piece])
                + (self.ring[0, last + piece] + self.ring[1, last + NP - 1 - piece]))

    def finish(self):
        def across(term, carry):
            self.mate_copy(term).wait_send()
            return carry
        terms = 2 * self.events + NP
        lax.fori_loop(terms - self.SLOTS, terms, across, 0)

        def ring(event, carry):
            self.ring_copy(event, 0).wait_send()
            self.ring_copy(event, 1).wait_send()
            return carry
        lax.fori_loop(self.events + 2 - (self.DEPTH - 1), self.events, ring, 0)

    def run(self, filler):
        def body(turn, carry):
            event = jnp.maximum(turn - 1, 0)
            travels = (turn >= 1) & (turn <= self.events)

            @pl.when(travels)
            def _():
                self.event(event)

            def ahead(way, inner):
                self.fill(2 * turn + way)
                return inner
            lax.fori_loop(0, 2, ahead, 0)

            @pl.when(travels)
            def _():
                filler(event)
            return carry
        lax.fori_loop(0, self.events + 2, body, 0)


def rope_pair(table):
    lanes = lax.broadcasted_iota(jnp.int32, table.shape, 1)
    swapped = pltpu.roll(table, HEAD_DIM // 2, 1)
    low = lanes < HEAD_DIM // 2
    return jnp.where(low, table, swapped), jnp.where(low, -swapped, table)


def fill_table(freqs, table_ref):
    rows = 64
    blocks = table_ref.shape[0] // rows

    def cos_sin(count, scale):
        steps = lax.broadcasted_iota(jnp.int32, (count, HEAD_DIM), 0) * scale
        angles = steps.astype(F32) * freqs
        return jnp.cos(angles), jnp.sin(angles)
    cos_low, sin_low = cos_sin(rows, 1)
    cos_high, sin_high = cos_sin(max(blocks, 8), rows)
    low = lax.broadcasted_iota(jnp.int32, (1, HEAD_DIM), 1) < HEAD_DIM // 2
    first = jnp.where(low, cos_high, sin_high)
    second = jnp.where(low, -sin_high, cos_high)
    for block in range(blocks):
        table_ref[block * rows:(block + 1) * rows] = first[block:block + 1] * cos_low + second[block:block + 1] * sin_low


def rope(values, table, inverse=False):
    cos2, sin2 = rope_pair(table)
    turned = pltpu.roll(values, HEAD_DIM // 2, 1)
    if inverse:
        return values * cos2 - turned * sin2
    return values * cos2 + turned * sin2


def norm_forward(x_f32, gain_row):
    inv = lax.rsqrt(jnp.mean(x_f32 * x_f32, axis=-1, keepdims=True) + NORM_EPS)
    return (x_f32 * inv * gain_row).astype(BF16)


def norm_backward(x_f32, gain_row, d_normed):
    inv = lax.rsqrt(jnp.mean(x_f32 * x_f32, axis=-1, keepdims=True) + NORM_EPS)
    unit = x_f32 * inv
    d_unit = d_normed * gain_row
    d_x = inv * (d_unit - unit * jnp.mean(d_unit * unit, axis=-1, keepdims=True))
    return d_x, jnp.sum(d_normed * unit, axis=0, keepdims=True)


def attention_block(row0, rows, keys, refs, forward, backward):
    q_ref, k_ref, v_ref, table_ref, read_da, write_o, dx_ref, dk_ref, dv_ref = refs
    here = pl.ds(aligned(row0, rows), rows)
    scale = HEAD_DIM ** -0.5
    query = q_ref[here]
    scores = dot_nt(query, k_ref[0:keys]) * scale
    row_id = row0 + lax.broadcasted_iota(jnp.int32, scores.shape, 0)
    col_id = lax.broadcasted_iota(jnp.int32, scores.shape, 1)
    scores = jnp.where(row_id >= col_id, scores, -1e30)
    expd = jnp.exp(scores - jnp.max(scores, axis=-1, keepdims=True))
    prob = expd * (1.0 / jnp.sum(expd, axis=-1, keepdims=True))
    prob_b = prob.astype(BF16)
    d_attn = read_da(here) if backward else None
    if forward:
        write_o(here, dot_nn(prob_b, v_ref[0:keys]).astype(BF16))
    if backward:
        dv_ref[0:keys] += dot_tn(prob_b, d_attn)
        d_prob = dot_nt(d_attn, v_ref[0:keys]).astype(BF16).astype(F32)
        row_dot = jnp.sum(prob * d_prob, axis=-1, keepdims=True)
        d_scores = (prob * (d_prob - row_dot) * scale).astype(BF16)
        d_query = dot_nn(d_scores, k_ref[0:keys]).astype(BF16).astype(F32)
        dx_ref[here, 0:HEAD_DIM] = rope(d_query, table_ref[here], inverse=True).astype(BF16)
        dk_ref[0:keys] += dot_tn(d_scores, query)


def store_keys_values(dx_ref, dk_ref, dv_ref, table_ref, rows):
    def body(block, carry):
        here = pl.ds(aligned(block * rows, rows), rows)
        d_key = dk_ref[here].astype(BF16).astype(F32)
        dx_ref[here, HEAD_DIM:2 * HEAD_DIM] = rope(d_key, table_ref[here], inverse=True).astype(BF16)
        dx_ref[here, 2 * HEAD_DIM:3 * HEAD_DIM] = dv_ref[here].astype(BF16)
        return carry
    lax.fori_loop(0, dx_ref.shape[0] // rows, body, 0)


def gated_pull(gate, up, d_hidden):
    sig = jax.nn.sigmoid(gate)
    silu = gate * sig
    d_silu = d_hidden * up
    return (silu * up).astype(BF16), (d_silu * sig + d_silu * silu * (1.0 - sig)).astype(BF16), (d_hidden * silu).astype(BF16)


class Copies:
    def __init__(self, sems):
        self.sems, self.used = sems, 0

    def start(self, src, dst):
        copy = pltpu.make_async_copy(src, dst, self.sems.at[self.used])
        self.used += 1
        copy.start()
        return copy


def gather_loop(gather, unit, then=None):
    chips = gather.place.ring

    def body(event, carry):
        @pl.when(event < gather.events)
        def _():
            gather.event(event)
            if then is not None:
                then(event)
        step = lax.div(event, NP) + 1
        opposite = event == gather.events
        final = event == gather.events - 1
        own = event == 1
        near = (event >= NP) & (event < gather.events) & (lax.rem(event, 2) == 0)

        @pl.when(opposite)
        def _():
            gather.mate_wait_last()

        @pl.when(own | near | final)
        def _():
            gather.mate_wait_chip(step - 1, final | (lax.rem(event, NP) != 0))

        @pl.when(own | near | final | opposite)
        def _():
            distance = lax.select(opposite, gather.place.half, step - 1)
            rightward = final | (lax.rem(event, NP) != 0)
            count = lax.select(own, 0, lax.select(opposite, chips - 1, lax.select(final, chips - 2, jnp.maximum(lax.div(event, 2) - 1, 0))))
            unit(count, gather.place.near(lax.select(rightward, distance, -distance)))
        return carry
    lax.fori_loop(0, gather.events + 1, body, 0)


def weight_grads_u(block, u_ref, dx_ref, stage_ref, outs, sems, head_cols, ff):
    rows = stage_ref.shape[1]
    slot = lax.rem(block, 2)
    here = pl.ds(aligned(block * rows, rows), rows)

    def copies():
        bounds = (0, head_cols, head_cols + ff, head_cols + 2 * ff)
        return [pltpu.make_async_copy(stage_ref.at[slot, :, bounds[i]:bounds[i + 1]], outs[i].at[here], sems.at[slot, i]) for i in range(3)]

    @pl.when(block >= 2)
    def _():
        for copy in copies():
            copy.wait()
    stage_ref[slot] = dot_tn(u_ref[:, here], dx_ref[...]).astype(BF16)
    for copy in copies():
        copy.start()


def weight_grads_u_wait(stage_ref, outs, sems, head_cols, ff):
    rows = stage_ref.shape[1]
    bounds = (0, head_cols, head_cols + ff, head_cols + 2 * ff)
    for slot in range(2):
        for i in range(3):
            pltpu.make_async_copy(stage_ref.at[slot, :, bounds[i]:bounds[i + 1]], outs[i].at[pl.ds(0, rows)], sems.at[slot, i]).wait()


def weight_grads_h(piece, ho_ref, read_dy, stage_ref, outs, sems, ff):
    cols = stage_ref.shape[2]
    stage_ref[piece] = dot_tn(ho_ref[...], read_dy(piece)).astype(BF16)
    for copy in h_copies(piece, stage_ref, outs, sems, ff):
        copy.start()


def h_copies(piece, stage_ref, outs, sems, ff):
    cols = stage_ref.shape[2]
    there = pl.ds(aligned(piece * cols, cols), cols)
    return [pltpu.make_async_copy(stage_ref.at[piece, 0:HEAD_DIM], outs[0].at[:, there], sems.at[piece, 0]),
            pltpu.make_async_copy(stage_ref.at[piece, HEAD_DIM:HEAD_DIM + ff], outs[1].at[:, there], sems.at[piece, 1])]


def kernel_main(tp_size, x_ref, gain_ref, freq_ref, gy_hbm, wqkv_hbm, wout_hbm, wgate_hbm, wup_hbm, wdown_hbm,
                dx_out, gain_out, *refs):
    firsts, lasts = refs[0:5], refs[5:10]
    u0_hbm, q_hbm, k_hbm, v_hbm, o_hbm, ab_hbm = refs[10:16]
    (u_ref, g_ref, wc_ref, wo_ref, q_ref, k_ref, v_ref, ho_ref, dx_ref, dk_ref, dv_ref, table_ref, x1_ref, gs_ref,
     pair_ref, all_ref, local, sems_gs, sems_hs, sem_ps, sem_pr, sem_as, sem_ar, free_sem) = refs[16:40]
    sems_u, sems_g, refs_r = refs[40:46], refs[46:52], refs[52:]
    place = Place(tp_size)
    shard, width = x_ref.shape
    pair = 2 * shard
    chips = place.ring
    head_cols = wqkv_hbm.shape[2]
    ff = wgate_hbm.shape[2]
    piece_cols = width // NP
    gate_cols = slice(head_cols, head_cols + ff)
    up_cols = slice(head_cols + ff, head_cols + 2 * ff)
    hidden_cols = slice(HEAD_DIM, HEAD_DIM + ff)
    loads = Copies(local)
    gu = Gather(place, u_ref, shard, sems_u)
    gg = Gather(place, g_ref, shard, sems_g)

    def wait_all(copies):
        for copy in copies:
            copy.wait()

    def load_wc(layer):
        return [loads.start(wqkv_hbm.at[layer], wc_ref.at[:, 0:head_cols]),
                loads.start(wgate_hbm.at[layer], wc_ref.at[:, gate_cols]),
                loads.start(wup_hbm.at[layer], wc_ref.at[:, up_cols])]

    def load_wo(layer):
        copies = []
        for piece in range(NP):
            cols = slice(piece * piece_cols, (piece + 1) * piece_cols)
            copies.append(loads.start(wout_hbm.at[layer, :, cols], wo_ref.at[piece, 0:HEAD_DIM]))
            copies.append(loads.start(wdown_hbm.at[layer, :, cols], wo_ref.at[piece, hidden_cols]))
        return copies

    def rows_of(chip):
        return pl.ds(aligned(chip * pair, pair), pair)

    def write_o(here, value):
        ho_ref[here, 0:HEAD_DIM] = value

    def read_da(here):
        return dx_ref[here, 0:HEAD_DIM]

    def heads(here, rows_u):
        qkv = dot_nn(rows_u, wc_ref[:, 0:head_cols]).astype(BF16)
        table = table_ref[here]
        q_ref[here] = rope(qkv[:, 0:HEAD_DIM].astype(F32), table).astype(BF16)
        k_ref[here] = rope(qkv[:, HEAD_DIM:2 * HEAD_DIM].astype(F32), table).astype(BF16)
        v_ref[here] = qkv[:, 2 * HEAD_DIM:3 * HEAD_DIM]

    def forward_unit(count, chip, with_hidden):
        here = rows_of(chip)
        rows_u = u_ref[here]
        heads(here, rows_u)
        gate = dot_nn(rows_u, wc_ref[:, gate_cols]).astype(BF16)
        up = dot_nn(rows_u, wc_ref[:, up_cols]).astype(BF16)
        dx_ref[here, gate_cols] = gate
        dx_ref[here, up_cols] = up
        if with_hidden:
            gate_f, up_f = gate.astype(F32), up.astype(F32)
            ho_ref[here, hidden_cols] = (gate_f * jax.nn.sigmoid(gate_f) * up_f).astype(BF16)

    def backward_unit(count, chip):
        here = rows_of(chip)
        dah = dot_nt(g_ref[here, 0:piece_cols], wo_ref[0])
        for piece in range(1, NP):
            dah = dah + dot_nt(g_ref[here, piece * piece_cols:(piece + 1) * piece_cols], wo_ref[piece])
        dx_ref[here, 0:HEAD_DIM] = dah[:, 0:HEAD_DIM].astype(BF16)
        d_hidden = dah[:, hidden_cols].astype(BF16).astype(F32)
        hidden, d_gate, d_up = gated_pull(dx_ref[here, gate_cols].astype(F32), dx_ref[here, up_cols].astype(F32), d_hidden)
        ho_ref[here, hidden_cols] = hidden
        dx_ref[here, gate_cols] = d_gate
        dx_ref[here, up_cols] = d_up

    def part_forward(chip, piece):
        return dot_nn(ho_ref[rows_of(chip)], wo_ref[piece])

    def part_backward(chip, piece):
        return dot_nt(dx_ref[rows_of(chip)], wc_ref[pl.ds(aligned(piece * piece_cols, piece_cols), piece_cols)])

    def read_dy(piece):
        return g_ref[:, pl.ds(aligned(piece * piece_cols, piece_cols), piece_cols)]

    def finals(reduce):
        return jnp.concatenate([reduce.final(piece) for piece in range(NP)], axis=1)

    def grads_filler(event, outs):
        outs_u, outs_h = (outs[0], outs[2], outs[3]), (outs[1], outs[4])

        @pl.when(event < NP)
        def _():
            weight_grads_h(event, ho_ref, read_dy, wo_ref, outs_h, sems_hs, ff)

        @pl.when((event >= NP) & (event < NP + chips))
        def _():
            weight_grads_u(jnp.maximum(event - NP, 0), u_ref, dx_ref, gs_ref, outs_u, sems_gs, head_cols, ff)

    def grads_wait(outs):
        outs_u, outs_h = (outs[0], outs[2], outs[3]), (outs[1], outs[4])
        for piece in range(NP):
            wait_all(h_copies(piece, wo_ref, outs_h, sems_hs, ff))
        weight_grads_u_wait(gs_ref, outs_u, sems_gs, head_cols, ff)

    def keep_gain(layer, row):
        lanes = all_ref.shape[2]
        tiles = width // lanes
        for tile in range(tiles):
            pair_ref[0, layer * tiles + tile:layer * tiles + tile + 1] = row[:, tile * lanes:(tile + 1) * lanes]

    load_g = loads.start(gy_hbm, g_ref.at[gg.own_rows()])
    load_w = load_wc(0)
    load_o = load_wo(0)
    u_ref[gu.own_rows()] = norm_forward(x_ref[...].astype(F32), gain_ref[0:1])
    place.barrier([{'tp': place.near(step) * 2 + place.core} for step in range(2, chips - 1)])
    gu.start()
    saves = [loads.start(u_ref.at[gu.own_rows()], u0_hbm)]
    fill_table(freq_ref[0:1], table_ref)
    load_g.wait()
    wait_all(load_w)

    def start_gy(event):
        @pl.when(event == gu.events - NP)
        def _():
            gg.start()
    gather_loop(gu, lambda count, chip: forward_unit(count, chip, True), start_gy)

    load_w = load_wc(1)
    saves += [loads.start(q_ref, q_hbm), loads.start(k_ref, k_hbm), loads.start(v_ref, v_hbm),
              loads.start(dx_ref.at[:, head_cols:head_cols + 2 * ff], ab_hbm)]

    def attend_first(block, carry):
        attention_block(block * pair, pair, chips * pair, (q_ref, k_ref, v_ref, table_ref, None, write_o, None, None, None), True, False)
        return carry
    lax.fori_loop(0, chips, attend_first, 0)
    saves += [loads.start(ho_ref.at[:, 0:HEAD_DIM], o_hbm)]
    wait_all(load_o)
    gu.finish()
    reduce = Reduce(place, part_forward, shard, refs_r)
    reduce.run(lambda event: None)
    load_o = load_wo(1)
    gg.event(jnp.int32(0), forward=True)
    gg.event(jnp.int32(1), forward=True)
    x_next = (x_ref[...].astype(F32) + finals(reduce)).astype(BF16)
    x1_ref[...] = x_next
    saves[0].wait()
    u_ref[gu.own_rows()] = norm_forward(x_next.astype(F32), gain_ref[1:2])

    reduce.finish()
    gu.start()
    wait_all(saves[1:])
    wait_all(load_w)
    wait_all(load_o)
    dk_ref[...] = jnp.zeros_like(dk_ref)
    dv_ref[...] = jnp.zeros_like(dv_ref)
    early = 2

    def more_gy(event):
        @pl.when(event >= gu.events - NP)
        def _():
            gg.event(jnp.maximum(event - (gu.events - NP), 0) + early, forward=True)
    gather_loop(gu, lambda count, chip: forward_unit(count, chip, False), more_gy)

    groups = 4

    def attend_last(turn, carry):
        held = early + NP
        distance = lax.div(turn + 1, 2)
        rightward = (turn > 0) & (lax.rem(turn, 2) == 0)
        opposite = turn == chips - 1
        needed = lax.select(turn == 0, held, lax.select(opposite, gg.events, distance * NP))
        begin = lax.select(turn == 0, held, jnp.minimum(jnp.maximum(held + turn - 1, lax.select(turn >= chips - 2, gg.events - NP // 2, 0)), gg.events))
        end = jnp.maximum(jnp.minimum(held + turn, gg.events), needed)
        end = lax.select(turn == chips - 2, jnp.maximum(end, gg.events - 1), end)
        begin = lax.select(turn == chips - 1, gg.events - 1, begin)

        def take(event, inner):
            gg.event(event)
            return inner
        lax.fori_loop(begin, end, take, 0)

        @pl.when(opposite)
        def _():
            gg.mate_wait_last()

        @pl.when(jnp.logical_not(opposite))
        def _():
            gg.mate_wait_chip(distance, rightward)
        chip = place.near(lax.select(rightward, distance, -distance))
        backward_unit(turn, chip)
        for group in range(groups):
            @pl.when(lax.div(chip, chips // groups) == group)
            def _(group=group):
                attention_block(chip * pair, pair, (group + 1) * (chips * pair // groups),
                                (q_ref, k_ref, v_ref, table_ref, read_da, write_o, dx_ref, dk_ref, dv_ref), True, True)
        return carry
    lax.fori_loop(0, chips, attend_last, 0)
    store_keys_values(dx_ref, dk_ref, dv_ref, table_ref, pair)
    gu.finish()
    gg.finish()
    loads_a = [loads.start(q_hbm, q_ref), loads.start(k_hbm, k_ref), loads.start(v_hbm, v_ref)]
    n_late = loads.used
    loads.used += 2

    def late_loads():
        return [pltpu.make_async_copy(u0_hbm, u_ref.at[gu.own_rows()], local.at[n_late]),
                pltpu.make_async_copy(o_hbm, ho_ref.at[:, 0:HEAD_DIM], local.at[n_late + 1])]
    near = (place.left, place.right, place.mate)
    reduce = Reduce(place, part_backward, shard, refs_r)

    def filler_last(event):
        grads_filler(event, lasts)

        @pl.when(event == NP + chips)
        def _():
            for copy in late_loads():
                copy.start()
            for peer in near:
                pl.semaphore_signal(free_sem, inc=1, device_id=peer, device_id_type=MESH)
    reduce.run(filler_last)
    pl.semaphore_wait(free_sem, len(near))
    wait_all(late_loads())
    gu.start()
    d_x, gain_row = norm_backward(x1_ref[...].astype(F32), gain_ref[1:2], finals(reduce).astype(BF16).astype(F32))
    g_ref[gg.own_rows()] = (g_ref[gg.own_rows()].astype(F32) + d_x).astype(BF16)
    keep_gain(1, gain_row)

    reduce.finish()
    gg.start()
    grads_wait(lasts)
    load_o = load_wo(0) + [loads.start(ab_hbm, dx_ref.at[:, head_cols:head_cols + 2 * ff])]
    load_w = load_wc(0)
    dk_ref[...] = jnp.zeros_like(dk_ref)
    dv_ref[...] = jnp.zeros_like(dv_ref)
    wait_all(load_o)

    def more_u(event):
        @pl.when(event >= gg.events - NP)
        def _():
            gu.event(jnp.maximum(event - (gg.events - NP), 0), forward=True)
    gather_loop(gg, backward_unit, more_u)
    wait_all(loads_a)

    def attend_back(block, carry):
        @pl.when(block < gu.events - 2 * NP)
        def _():
            gu.event(block + NP, forward=True)

        def body(sub, inner):
            attention_block((block * 2 + sub) * shard, shard, chips * pair,
                            (q_ref, k_ref, v_ref, table_ref, read_da, None, dx_ref, dk_ref, dv_ref), False, True)
            return inner
        lax.fori_loop(0, 2, body, 0)
        return carry
    lax.fori_loop(0, chips, attend_back, 0)
    store_keys_values(dx_ref, dk_ref, dv_ref, table_ref, pair)
    wait_all(load_w)
    reduce = Reduce(place, part_backward, shard, refs_r)

    def filler_first(event):
        @pl.when(event < NP)
        def _():
            gu.event(gu.events - NP + event, forward=False)

        @pl.when(event == NP - 1)
        def _():
            gu.mate_wait_all()
        grads_filler(event, firsts)
    reduce.run(filler_first)
    d_x, gain_row = norm_backward(x_ref[...].astype(F32), gain_ref[0:1], finals(reduce).astype(BF16).astype(F32))
    keep_gain(0, gain_row)

    cross = pltpu.make_async_remote_copy(pair_ref.at[0], pair_ref.at[1], sem_ps, sem_pr, place.mate, MESH)
    cross.start()
    dx_out[...] = (g_ref[gg.own_rows()].astype(F32) + d_x).astype(BF16)
    cross.wait()
    all_ref[place.chip] = pair_ref[0] + pair_ref[1]

    def spread(step):
        return pltpu.make_async_remote_copy(
            all_ref.at[place.chip], all_ref.at[place.chip], sem_as.at[step - 1], sem_ar.at[step - 1],
            {'tp': place.near(step) * 2 + place.core}, MESH)
    for step in range(1, chips):
        spread(step).start()
    gu.finish()
    gg.finish()
    reduce.finish()
    grads_wait(firsts)
    for step in range(1, chips):
        spread(step).wait()
    total = all_ref[0]
    for chip in range(1, chips):
        total = total + all_ref[chip]
    lanes = total.shape[1]
    tiles = width // lanes
    for tile in range(tiles):
        for layer in range(2):
            gain_out[layer:layer + 1, tile * lanes:(tile + 1) * lanes] = total[layer * tiles + tile:layer * tiles + tile + 1]


def kernel_stack(*refs):
    lasts, firsts, rest, outs, out_rest = refs[0:5], refs[5:10], refs[10:12], refs[12:17], refs[17:19]
    bufs, buf_rest, (sem_in, sem_out) = refs[19:24], refs[24:26], refs[26:28]
    steps = [(source, bufs[number].at[layer], outs[number].at[layer])
             for layer, sources in ((1, lasts), (0, firsts)) for number, source in enumerate(sources)]
    steps += list(zip(rest, buf_rest, out_rest))
    reads = [pltpu.make_async_copy(source, buf, sem_in.at[slot]) for slot, (source, buf, out) in enumerate(steps)]
    writes = [pltpu.make_async_copy(buf, out, sem_out.at[slot]) for slot, (source, buf, out) in enumerate(steps)]
    for read in reads:
        read.start()
    for read, write in zip(reads, writes):
        read.wait()
        write.start()
    for write in writes:
        write.wait()


def solution(mesh):
    tp_size = mesh.shape['tp']
    half = tp_size // 4
    row_spec = P(('dp', 'tp'), None)
    col_spec = P(None, None, 'tp')
    inner_spec = P(None, 'tp', None)

    def device_program(x_loc, dy_loc, norm_gain, w_qkv, w_out, w_gate, w_up, w_down):
        shard, width = x_loc.shape
        seq = shard * tp_size
        pair = 2 * shard
        chips = tp_size // 2
        head_cols = w_qkv.shape[2]
        ff = w_gate.shape[2]
        cols = head_cols + 2 * ff
        piece_cols = width // NP
        vmem, anyspace = pl.BlockSpec(memory_space=pltpu.VMEM), pl.BlockSpec(memory_space=pl.ANY)
        shape = jax.ShapeDtypeStruct
        dma = pltpu.SemaphoreType.DMA

        freqs = np.float32(ROPE_BASE) ** (np.float32(-2.0) * np.arange(HEAD_DIM // 2, dtype=np.float32) / np.float32(HEAD_DIM))
        freqs = jnp.asarray(np.tile(freqs, (8, 2)))

        rows_shape = shape((shard, width), BF16)
        gain_shape = shape((2, width), F32)
        head_shape = shape((seq, HEAD_DIM), BF16)
        grads = (shape((width, head_cols), BF16), shape((HEAD_DIM, width), BF16), shape((width, ff), BF16),
                 shape((width, ff), BF16), shape((ff, width), BF16))
        whole_vmem = 67043328
        results = pl.pallas_call(
            functools.partial(kernel_main, tp_size),
            out_shape=(rows_shape, gain_shape) + grads + grads + (rows_shape,) + (head_shape,) * 4 + (shape((seq, 2 * ff), BF16),),
            in_specs=[vmem] * 3 + [anyspace] * 6,
            out_specs=(vmem, vmem) + (anyspace,) * 16,
            scratch_shapes=[
                pltpu.VMEM((seq, width), BF16), pltpu.VMEM((seq, width), BF16), pltpu.VMEM((width, cols), BF16),
                pltpu.VMEM((NP, HEAD_DIM + ff, piece_cols), BF16),
                pltpu.VMEM((seq, HEAD_DIM), BF16), pltpu.VMEM((seq, HEAD_DIM), BF16), pltpu.VMEM((seq, HEAD_DIM), BF16),
                pltpu.VMEM((seq, HEAD_DIM + ff), BF16), pltpu.VMEM((seq, cols), BF16),
                pltpu.VMEM((seq, HEAD_DIM), F32), pltpu.VMEM((seq, HEAD_DIM), F32), pltpu.VMEM((seq, HEAD_DIM), F32),
                pltpu.VMEM((shard, width), BF16), pltpu.VMEM((2, width // chips, cols), BF16),
                pltpu.VMEM((2, 2 * width // 128, 128), F32), pltpu.VMEM((chips, 2 * width // 128, 128), F32),
                dma((64,)), dma((2, 3)), dma((NP, 2)), dma(()), dma(()), dma((chips - 1,)), dma((chips - 1,)),
                pltpu.SemaphoreType.REGULAR] + Gather.scratch(half) + Gather.scratch(half) + Reduce.scratch(half, shard, piece_cols),
            compiler_params=pltpu.CompilerParams(collective_id=1, has_side_effects=True, vmem_limit_bytes=whole_vmem), name='blocks',
        )(x_loc, norm_gain, freqs, dy_loc, w_qkv, w_out, w_gate, w_up, w_down)

        stacked = pl.pallas_call(
            kernel_stack,
            out_shape=tuple(shape((2,) + grad.shape, BF16) for grad in grads) + (rows_shape, gain_shape),
            in_specs=[anyspace] * 12,
            out_specs=(anyspace,) * 7,
            scratch_shapes=[pltpu.VMEM((2,) + grad.shape, BF16) for grad in grads]
            + [pltpu.VMEM(rows_shape.shape, BF16), pltpu.VMEM(gain_shape.shape, F32), dma((12,)), dma((12,))],
            compiler_params=pltpu.CompilerParams(vmem_limit_bytes=whole_vmem), name='stack',
        )(*results[7:12], *results[2:7], *results[0:2])
        return tuple(stacked[5:7]) + tuple(stacked[0:5])

    return jax.shard_map(device_program, mesh=mesh, in_specs=(row_spec, row_spec, P(None, None), col_spec, inner_spec, col_spec, col_spec, inner_spec), out_specs=(row_spec, P('dp', None), P('dp', None, 'tp'), P('dp', 'tp', None), P('dp', None, 'tp'), P('dp', None, 'tp'), P('dp', 'tp', None)), check_vma=False)
```

time: 529 us -> 508 us (0.960)
  local copies, waits for them, and re-layouts: 12.7 us -> 0 us
  Pallas kernels: 515 us -> 507 us
    unnamed x22 -> x0, local copies, waits for them, and re-layouts: 12.7 us -> none
    pallas_call x4 -> x2, Pallas kernels: 515 us -> 507 us  [the longest x1 495 us: device_program(): pl.pallas_call(functools.partial(kernel_main, tp_size), out_shape=(rows_s...]
where the time goes in v3:
time: 508 us
  Pallas kernels  507 us (100%)
    pallas_call x1, Pallas kernels, device_program(): pl.pallas_call(functools.partial(kernel_main, tp_size), out_shape=(rows_s...  495 us
    pallas_call x1, Pallas kernels, device_program(): pl.pallas_call(kernel_stack, out_shape=tuple((shape((2,) + grad.shape, BF...  12.4 us

profile of v3, /device:TPU:21, one launch (start us, length us, event | category | flops | bytes accessed | tf_op | source)
XLA Modules:
  0.0 508.1 jit_solution(10044457410232594419)
XLA Ops:
  0.6 494.9 %blocks.1 = (bf16[128,2048]{1,0:T(8,128)(2,1)}, f32[2,2048]{1,0:T(2,128)}, bf16[2048,384]{1,0:T(8,128)(2,1)}, bf16[128,2048]{1,0:T(8,128)(2,1)}, bf16[2048,512]{...) custom-call(bf16[128,2048]{1,0:T(8,128)(2,1)} %x_ref.1, ...), custom_call_target="tpu_custom_call" | custom-call | tf_op jit(solution)/shard_map/blocks/pallas_call | solution.py:780
  495.6 12.4 %stack.1 = (bf16[2,2048,384]{2,1,0:T(8,128)(2,1)}, bf16[2,128,2048]{2,1,0:T(8,128)(2,1)}, bf16[2,2048,512]{2,1,0:T(8,128)(2,1)}, bf16[2,2048,512]{2,1,0:T(8,128)...) custom-call(bf16[2048,384]{1,0:T(8,128)(2,1)} %get-tuple-element.26.refs_0_, ...), custom_call_target="tpu_custom_call" | custom-call | tf_op jit(solution)/shard_map/stack/pallas_call | solution.py:798
